TPU v7x, 32 devices: a 4x2x2 block of a 4x4x8 slice. The times are simulated.
32 devices in a mesh: dp: 4 (over y, z), sp: 8 (over x, core).
Axes of the slice: x: 4, y: 2, z: 2, core: 2. Of those that a mesh axis runs over, the one named last changes fastest.
The devices are a block of a 4x4x8 slice.
Arguments:
- tok_in: bfloat16 [8192, 7168], P(('dp', 'sp')), parts along dimension 0
- tok_pos: int32 [8192], P(('dp', 'sp')), parts along dimension 0
- w_dq: bfloat16 [7168, 1536], replicated
- g_q: float32 [1536], replicated
- w_uq: bfloat16 [1536, 128, 192], replicated
- w_dkv: bfloat16 [7168, 576], replicated
- g_kv: float32 [512], replicated
- w_uk: bfloat16 [512, 128, 128], replicated
- w_uv: bfloat16 [512, 128, 128], replicated
- w_o: bfloat16 [128, 128, 7168], replicated
Outputs:
- output 1: bfloat16 [8192, 7168], P(('dp', 'sp')), parts along dimension 0
- output 2: bfloat16 [8192, 512], P(('dp', 'sp')), parts along dimension 0
- output 3: bfloat16 [8192, 64], P(('dp', 'sp')), parts along dimension 0
There are 4 independent parts. A program takes and returns all parts, laid end to end along the dimension named above; an argument that names none is the same for every part.
All inputs are finite; a program needn't handle non-finite values.
Results may differ from a plain program's by a relative error of at most 0.00551604.
Values are sent between devices in bfloat16 or wider.
A program may use at most 768 MiB of HBM per device.

v0:
```python
import math
import jax
import jax.numpy as jnp
from jax import lax
from jax.sharding import PartitionSpec as P

ROPE_THETA = 10000.0
YARN_FACTOR = 40.0
ORIG_CTX = 4096.0
BETA_FAST = 32.0
BETA_SLOW = 1.0
NORM_EPS = 1e-6


def rope_freqs(rot_dim):
    half_dim = rot_dim // 2
    log_base = 2.0 * math.log(ROPE_THETA)
    low_idx = max(math.floor(rot_dim * math.log(ORIG_CTX / (BETA_FAST * 2.0 * math.pi)) / log_base), 0)
    high_idx = min(math.ceil(rot_dim * math.log(ORIG_CTX / (BETA_SLOW * 2.0 * math.pi)) / log_base), half_dim - 1)
    spread = max(high_idx - low_idx, 0.001)
    freq_list = []
    for freq_idx in range(half_dim):
        base_freq = ROPE_THETA ** (-2.0 * freq_idx / rot_dim)
        ramp_val = min(max((freq_idx - low_idx) / spread, 0.0), 1.0)
        freq_list.append(base_freq / YARN_FACTOR * ramp_val + base_freq * (1.0 - ramp_val))
    return jnp.asarray(freq_list, dtype=jnp.float32)


def rotate_half(act_in, cos_t, sin_t):
    half_dim = act_in.shape[-1] // 2
    first = act_in[..., :half_dim]
    second = act_in[..., half_dim:]
    return jnp.concatenate([first * cos_t - second * sin_t, second * cos_t + first * sin_t], axis=-1)


def rms_norm(act_in, gain):
    mean_sq = jnp.mean(act_in * act_in, axis=-1, keepdims=True)
    return act_in * lax.rsqrt(mean_sq + NORM_EPS) * gain


def solution(mesh):
    groups = mesh.shape['sp']
    tok_spec = P(('dp', 'sp'))
    rows_spec = P(('dp', 'sp'), None)
    replicated = P()

    def local_step(tok_in, tok_pos, w_dq, g_q, w_uq, w_dkv, g_kv, w_uk, w_uv, w_o):
        rows = tok_in.shape[0]
        num_heads = w_uq.shape[1]
        qk_dim = w_uq.shape[2]
        kv_rank = g_kv.shape[0]
        rot_dim = w_dkv.shape[1] - kv_rank
        nope_dim = qk_dim - rot_dim
        v_dim = w_uv.shape[2]
        seq_len = rows * groups
        attn_scale = (0.1 * math.log(YARN_FACTOR) + 1.0) ** 2 / math.sqrt(qk_dim)
        angles = tok_pos.astype(jnp.float32)[:, None] * rope_freqs(rot_dim)[None, :]
        cos_t = jnp.cos(angles)
        sin_t = jnp.sin(angles)
        q_lat = rms_norm(jnp.dot(tok_in, w_dq, preferred_element_type=jnp.float32), g_q).astype(jnp.bfloat16)
        q_full = jnp.einsum('tc,che->the', q_lat, w_uq, preferred_element_type=jnp.float32)
        q_all = jnp.concatenate([q_full[:, :, :nope_dim], rotate_half(q_full[:, :, nope_dim:], cos_t[:, None, :], sin_t[:, None, :])], axis=-1).astype(jnp.bfloat16)
        kv_lat = jnp.dot(tok_in, w_dkv, preferred_element_type=jnp.float32)
        cache_kv = rms_norm(kv_lat[:, :kv_rank], g_kv).astype(jnp.bfloat16)
        cache_pe = rotate_half(kv_lat[:, kv_rank:], cos_t, sin_t).astype(jnp.bfloat16)
        k_nope = jnp.einsum('tc,chn->thn', cache_kv, w_uk, preferred_element_type=jnp.float32).astype(jnp.bfloat16)
        values = jnp.einsum('tc,chv->thv', cache_kv, w_uv, preferred_element_type=jnp.float32).astype(jnp.bfloat16)
        k_all = jnp.concatenate([k_nope, jnp.broadcast_to(cache_pe[:, None, :], (rows, num_heads, rot_dim))], axis=-1)
        q_heads = lax.all_to_all(q_all, 'sp', 1, 0, tiled=True)
        k_heads = lax.all_to_all(k_all, 'sp', 1, 0, tiled=True)
        v_heads = lax.all_to_all(values, 'sp', 1, 0, tiled=True)
        key_idx = jnp.arange(seq_len)

        def block_attention(blk_idx):
            start = blk_idx * rows
            q_blk = lax.dynamic_slice_in_dim(q_heads, start, rows, axis=0)
            logits = jnp.einsum('qhe,khe->hqk', q_blk, k_heads, preferred_element_type=jnp.float32) * attn_scale
            row_idx = start + jnp.arange(rows)
            logits = jnp.where(key_idx[None, None, :] <= row_idx[None, :, None], logits, -jnp.inf)
            attn_prob = jax.nn.softmax(logits, axis=-1).astype(jnp.bfloat16)
            return jnp.einsum('hqk,khv->qhv', attn_prob, v_heads, preferred_element_type=jnp.float32).astype(jnp.bfloat16)

        o_heads = lax.map(block_attention, jnp.arange(groups)).reshape(seq_len, num_heads // groups, v_dim)
        o_local = lax.all_to_all(o_heads, 'sp', 0, 1, tiled=True)
        attn_out = jnp.einsum('thv,hvd->td', o_local, w_o, preferred_element_type=jnp.float32).astype(jnp.bfloat16)
        return attn_out, cache_kv, cache_pe

    return jax.shard_map(local_step, mesh=mesh, in_specs=(rows_spec, tok_spec, replicated, replicated, replicated, replicated, replicated, replicated, replicated, replicated), out_specs=(rows_spec, rows_spec, rows_spec), check_vma=False)
```

profile of v0, /device:TPU:81, one launch (start us, length us, event | category | flops | bytes accessed | tf_op | source)
XLA Modules:
  0.0 939.0 jit_solution(9611396786545765574)
XLA Ops:
  7.7 21.3 %fusion.30 = bf16[256,128,128]{2,0,1:T(8,128)(2,1)} fusion(bf16[512,128,128]{2,1,0:T(8,128)(2,1)} %param.21, bf16[256,512]{0,1:T(8,128)(2,1)S(1)} %multiply_convert_fusion.1), kind=kOutput, calls=%fused_computation.32 | convolution fusion | flops 4299161600 | bytes 25427968 | tf_op jit(solution)/shard_map/tc,chv->thv/dot_general | solution.py:67
  47.4 54.3 %fusion.25 = f32[256,128,192]{1,0,2:T(8,128)} fusion(bf16[1536,128,192]{1,2,0:T(8,128)(2,1)} %param.17, f32[256,1536]{1,0:T(8,128)S(1)} %get-tuple-element.88, f32[1536]{0:T(1024)S(1)} %copy-done.6, f32[256]{0:T(256)S(1)} %add_rsqrt_fusion.1), kind=kOutput, calls=%fused_computation.23 | convolution fusion | flops 19328532480 | bytes 102243328 | tf_op jit(solution)/shard_map/tc,che->the/dot_general | solution.py:61
  122.0 17.0 %copy.47 = bf16[256,128,192]{0,2,1:T(8,128)(2,1)} copy(bf16[256,128,192]{1,0,2:T(8,128)(2,1)} %pad_maximum_fusion) | data formatting | bytes 25165824 | tf_op jit(solution)/shard_map/concatenate | solution.py:62
  144.6 24.3 %copy.50 = bf16[512,128,128]{0,2,1:T(8,128)(2,1)} copy(bf16[512,128,128]{2,1,0:T(8,128)(2,1)} %param.20) | data formatting | bytes 33554432 | tf_op args[7]
  188.2 94.9 %all-to-all-done = bf16[256,128,192]{0,2,1:T(8,128)(2,1)} async-done(((bf16[256,128,192]{0,2,1:T(8,128)(2,1)}), bf16[256,128,192]{0,2,1:T(8,128)(2,1)}, u32[]{:S(2)}, u32[]{:S(2)}) %all-to-all-start) | async-done | bytes 12582944 | tf_op jit(solution)/shard_map/all_to_all | solution.py:69
  308.0 120.0 %all-to-all-done.1 = bf16[256,128,192]{0,2,1:T(8,128)(2,1)} async-done(((bf16[256,128,192]{0,2,1:T(8,128)(2,1)}), bf16[256,128,192]{0,2,1:T(8,128)(2,1)}, u32[]{:S(2)}, u32[]{:S(2)}) %all-to-all-start.1) | async-done | bytes 12582944 | tf_op jit(solution)/shard_map/all_to_all | solution.py:70
  438.8 308.9 %while.11 = (s32[]{:T(128)}, bf16[8,256,16,128]{3,2,1,0:T(8,128)(2,1)}, s32[8]{0:T(128)S(1)}, bf16[2048,16,192]{0,2,1:T(8,128)(2,1)}, bf16[2048,16,192]{0,2,1:T(...) while((s32[]{:T(128)}, ...), condition=%wide.region_5.6_spmd.clone, body=%wide.region_2.5_spmd.clone.sunk | while | flops 5420091392 | bytes 93883048 | solution.py:83
  440.3 19.9 %fusion.64 = (f32[16,256]{1,0:T(8,128)S(1)}, f32[16,256,2048]{2,1,0:T(8,128)}) fusion(pred[256,2048]{1,0:T(8,128)(4,1)S(1)} %iota_compare_fusion.2, bf16[2048,16,192]{0,2,1:T(8,128)(2,1)} %get-tuple-element.154, bf16[2048,16,192]{0,2,1:T(8,128)(2,1)} %get-tuple-element.153, s32[]{:T(128)S(6)} %select_n.22), kind=kOutput, calls=%fused_computation.50.clone.1 | convolution fusion | flops 3254781952 | bytes 48250884 | tf_op jit(solution)/shard_map/while/body/eval_jaxpr/sub | solution.py:80
  460.3 15.5 %fusion.65 = bf16[1,256,16,128]{3,1,2,0:T(8,128)(2,1)S(1)} fusion(bf16[2048,16,128]{2,0,1:T(8,128)(2,1)} %get-tuple-element.155, f32[16,256,2048]{2,1,0:T(8,128)} %get-tuple-element.128, f32[16,256]{1,0:T(8,128)S(1)} %get-tuple-element.129), kind=kOutput, calls=%fused_computation.16.clone.1 | convolution fusion | flops 2164785152 | bytes 43008000 | tf_op jit(solution)/shard_map/while/body/eval_jaxpr/hqk,khv->qhv/dot_general | solution.py:81
  478.9 19.9 %fusion.64 = (f32[16,256]{1,0:T(8,128)S(1)}, f32[16,256,2048]{2,1,0:T(8,128)}) fusion(pred[256,2048]{1,0:T(8,128)(4,1)S(1)} %iota_compare_fusion.2, bf16[2048,16,192]{0,2,1:T(8,128)(2,1)} %get-tuple-element.154, bf16[2048,16,192]{0,2,1:T(8,128)(2,1)} %get-tuple-element.153, s32[]{:T(128)S(6)} %select_n.22), kind=kOutput, calls=%fused_computation.50.clone.1 | convolution fusion | flops 3254781952 | bytes 48250884 | tf_op jit(solution)/shard_map/while/body/eval_jaxpr/sub | solution.py:80
  498.8 15.5 %fusion.65 = bf16[1,256,16,128]{3,1,2,0:T(8,128)(2,1)S(1)} fusion(bf16[2048,16,128]{2,0,1:T(8,128)(2,1)} %get-tuple-element.155, f32[16,256,2048]{2,1,0:T(8,128)} %get-tuple-element.128, f32[16,256]{1,0:T(8,128)S(1)} %get-tuple-element.129), kind=kOutput, calls=%fused_computation.16.clone.1 | convolution fusion | flops 2164785152 | bytes 43008000 | tf_op jit(solution)/shard_map/while/body/eval_jaxpr/hqk,khv->qhv/dot_general | solution.py:81
  517.6 19.9 %fusion.64 = (f32[16,256]{1,0:T(8,128)S(1)}, f32[16,256,2048]{2,1,0:T(8,128)}) fusion(pred[256,2048]{1,0:T(8,128)(4,1)S(1)} %iota_compare_fusion.2, bf16[2048,16,192]{0,2,1:T(8,128)(2,1)} %get-tuple-element.154, bf16[2048,16,192]{0,2,1:T(8,128)(2,1)} %get-tuple-element.153, s32[]{:T(128)S(6)} %select_n.22), kind=kOutput, calls=%fused_computation.50.clone.1 | convolution fusion | flops 3254781952 | bytes 48250884 | tf_op jit(solution)/shard_map/while/body/eval_jaxpr/sub | solution.py:80
  537.5 15.5 %fusion.65 = bf16[1,256,16,128]{3,1,2,0:T(8,128)(2,1)S(1)} fusion(bf16[2048,16,128]{2,0,1:T(8,128)(2,1)} %get-tuple-element.155, f32[16,256,2048]{2,1,0:T(8,128)} %get-tuple-element.128, f32[16,256]{1,0:T(8,128)S(1)} %get-tuple-element.129), kind=kOutput, calls=%fused_computation.16.clone.1 | convolution fusion | flops 2164785152 | bytes 43008000 | tf_op jit(solution)/shard_map/while/body/eval_jaxpr/hqk,khv->qhv/dot_general | solution.py:81
  556.2 19.9 %fusion.64 = (f32[16,256]{1,0:T(8,128)S(1)}, f32[16,256,2048]{2,1,0:T(8,128)}) fusion(pred[256,2048]{1,0:T(8,128)(4,1)S(1)} %iota_compare_fusion.2, bf16[2048,16,192]{0,2,1:T(8,128)(2,1)} %get-tuple-element.154, bf16[2048,16,192]{0,2,1:T(8,128)(2,1)} %get-tuple-element.153, s32[]{:T(128)S(6)} %select_n.22), kind=kOutput, calls=%fused_computation.50.clone.1 | convolution fusion | flops 3254781952 | bytes 48250884 | tf_op jit(solution)/shard_map/while/body/eval_jaxpr/sub | solution.py:80
  594.8 19.9 %fusion.64 = (f32[16,256]{1,0:T(8,128)S(1)}, f32[16,256,2048]{2,1,0:T(8,128)}) fusion(pred[256,2048]{1,0:T(8,128)(4,1)S(1)} %iota_compare_fusion.2, bf16[2048,16,192]{0,2,1:T(8,128)(2,1)} %get-tuple-element.154, bf16[2048,16,192]{0,2,1:T(8,128)(2,1)} %get-tuple-element.153, s32[]{:T(128)S(6)} %select_n.22), kind=kOutput, calls=%fused_computation.50.clone.1 | convolution fusion | flops 3254781952 | bytes 48250884 | tf_op jit(solution)/shard_map/while/body/eval_jaxpr/sub | solution.py:80
  614.7 15.5 %fusion.65 = bf16[1,256,16,128]{3,1,2,0:T(8,128)(2,1)S(1)} fusion(bf16[2048,16,128]{2,0,1:T(8,128)(2,1)} %get-tuple-element.155, f32[16,256,2048]{2,1,0:T(8,128)} %get-tuple-element.128, f32[16,256]{1,0:T(8,128)S(1)} %get-tuple-element.129), kind=kOutput, calls=%fused_computation.16.clone.1 | convolution fusion | flops 2164785152 | bytes 43008000 | tf_op jit(solution)/shard_map/while/body/eval_jaxpr/hqk,khv->qhv/dot_general | solution.py:81
  633.4 19.9 %fusion.64 = (f32[16,256]{1,0:T(8,128)S(1)}, f32[16,256,2048]{2,1,0:T(8,128)}) fusion(pred[256,2048]{1,0:T(8,128)(4,1)S(1)} %iota_compare_fusion.2, bf16[2048,16,192]{0,2,1:T(8,128)(2,1)} %get-tuple-element.154, bf16[2048,16,192]{0,2,1:T(8,128)(2,1)} %get-tuple-element.153, s32[]{:T(128)S(6)} %select_n.22), kind=kOutput, calls=%fused_computation.50.clone.1 | convolution fusion | flops 3254781952 | bytes 48250884 | tf_op jit(solution)/shard_map/while/body/eval_jaxpr/sub | solution.py:80
  653.3 15.5 %fusion.65 = bf16[1,256,16,128]{3,1,2,0:T(8,128)(2,1)S(1)} fusion(bf16[2048,16,128]{2,0,1:T(8,128)(2,1)} %get-tuple-element.155, f32[16,256,2048]{2,1,0:T(8,128)} %get-tuple-element.128, f32[16,256]{1,0:T(8,128)S(1)} %get-tuple-element.129), kind=kOutput, calls=%fused_computation.16.clone.1 | convolution fusion | flops 2164785152 | bytes 43008000 | tf_op jit(solution)/shard_map/while/body/eval_jaxpr/hqk,khv->qhv/dot_general | solution.py:81
  672.0 19.9 %fusion.64 = (f32[16,256]{1,0:T(8,128)S(1)}, f32[16,256,2048]{2,1,0:T(8,128)}) fusion(pred[256,2048]{1,0:T(8,128)(4,1)S(1)} %iota_compare_fusion.2, bf16[2048,16,192]{0,2,1:T(8,128)(2,1)} %get-tuple-element.154, bf16[2048,16,192]{0,2,1:T(8,128)(2,1)} %get-tuple-element.153, s32[]{:T(128)S(6)} %select_n.22), kind=kOutput, calls=%fused_computation.50.clone.1 | convolution fusion | flops 3254781952 | bytes 48250884 | tf_op jit(solution)/shard_map/while/body/eval_jaxpr/sub | solution.py:80
  691.9 15.5 %fusion.65 = bf16[1,256,16,128]{3,1,2,0:T(8,128)(2,1)S(1)} fusion(bf16[2048,16,128]{2,0,1:T(8,128)(2,1)} %get-tuple-element.155, f32[16,256,2048]{2,1,0:T(8,128)} %get-tuple-element.128, f32[16,256]{1,0:T(8,128)S(1)} %get-tuple-element.129), kind=kOutput, calls=%fused_computation.16.clone.1 | convolution fusion | flops 2164785152 | bytes 43008000 | tf_op jit(solution)/shard_map/while/body/eval_jaxpr/hqk,khv->qhv/dot_general | solution.py:81
  710.6 19.9 %fusion.64 = (f32[16,256]{1,0:T(8,128)S(1)}, f32[16,256,2048]{2,1,0:T(8,128)}) fusion(pred[256,2048]{1,0:T(8,128)(4,1)S(1)} %iota_compare_fusion.2, bf16[2048,16,192]{0,2,1:T(8,128)(2,1)} %get-tuple-element.154, bf16[2048,16,192]{0,2,1:T(8,128)(2,1)} %get-tuple-element.153, s32[]{:T(128)S(6)} %select_n.22), kind=kOutput, calls=%fused_computation.50.clone.1 | convolution fusion | flops 3254781952 | bytes 48250884 | tf_op jit(solution)/shard_map/while/body/eval_jaxpr/sub | solution.py:80
  730.5 15.5 %fusion.65 = bf16[1,256,16,128]{3,1,2,0:T(8,128)(2,1)S(1)} fusion(bf16[2048,16,128]{2,0,1:T(8,128)(2,1)} %get-tuple-element.155, f32[16,256,2048]{2,1,0:T(8,128)} %get-tuple-element.128, f32[16,256]{1,0:T(8,128)S(1)} %get-tuple-element.129), kind=kOutput, calls=%fused_computation.16.clone.1 | convolution fusion | flops 2164785152 | bytes 43008000 | tf_op jit(solution)/shard_map/while/body/eval_jaxpr/hqk,khv->qhv/dot_general | solution.py:81
  755.1 92.6 %all-to-all-done.3 = bf16[2048,16,128]{2,1,0:T(8,128)(2,1)} async-done(((bf16[2048,16,128]{2,1,0:T(8,128)(2,1)}), bf16[2048,16,128]{2,1,0:T(8,128)(2,1)}, u32[]{:S(2)}, u32[]{:S(2)}) %all-to-all-start.3) | async-done | bytes 8388640 | tf_op jit(solution)/shard_map/all_to_all | solution.py:84
  856.7 81.9 %fusion.29 = bf16[256,7168]{1,0:T(8,128)(2,1)} fusion(bf16[256,128,128]{2,0,1:T(8,128)(2,1)} %bitcast.61, bf16[128,128,7168]{2,1,0:T(8,128)(2,1)} %param.22), kind=kOutput, calls=%fused_computation.31 | convolution fusion | flops 60131377152 | bytes 246939648 | tf_op jit(solution)/shard_map/thv,hvd->td/dot_general | solution.py:85
  (75 shorter events, 159.0 us)
Async XLA Ops:
  0.6 6.9 copy-start.3
  7.7 161.2 %copy-start = (bf16[256,512]{0,1:T(8,128)(2,1)}, bf16[256,512]{0,1:T(8,128)(2,1)S(1)}, u32[]{:S(2)}) copy-start(bf16[256,512]{0,1:T(8,128)(2,1)S(1)} %multiply_convert_fusion.1) | copy-start | bytes 786436
  29.0 110.0 %all-to-all-start.2 = ((bf16[256,128,128]{2,0,1:T(8,128)(2,1)}), bf16[256,128,128]{2,0,1:T(8,128)(2,1)}, u32[]{:S(2)}, u32[]{:S(2)}) async-start(bf16[256,128,128]{2,0,1:T(8,128)(2,1)} %fusion.30), calls=%async_computation.2 | async-start | bytes 16777216 | tf_op jit(solution)/shard_map/all_to_all | solution.py:71
  35.9 11.4 %copy-start.4 = (s32[256]{0:T(256)S(1)}, s32[256]{0:T(256)}, u32[]{:S(2)}) copy-start(s32[256]{0:T(256)} %param.14) | copy-start | bytes 3076
  35.9 11.5 %copy-start.6 = (f32[1536]{0:T(1024)S(1)}, f32[1536]{0:T(1024)}, u32[]{:S(2)}) copy-start(f32[1536]{0:T(1024)} %param.16) | copy-start | bytes 18436
  101.6 6.6 copy-start.5
  139.0 144.1 %all-to-all-start = ((bf16[256,128,192]{0,2,1:T(8,128)(2,1)}), bf16[256,128,192]{0,2,1:T(8,128)(2,1)}, u32[]{:S(2)}, u32[]{:S(2)}) async-start(bf16[256,128,192]{0,2,1:T(8,128)(2,1)} %copy.47), calls=%async_computation | async-start | bytes 25165824 | tf_op jit(solution)/shard_map/all_to_all | solution.py:69
  178.3 0.6 copy-start.2
  283.1 144.8 %all-to-all-start.1 = ((bf16[256,128,192]{0,2,1:T(8,128)(2,1)}), bf16[256,128,192]{0,2,1:T(8,128)(2,1)}, u32[]{:S(2)}, u32[]{:S(2)}) async-start(bf16[256,128,192]{0,2,1:T(8,128)(2,1)} %pad_maximum_fusion.1), calls=%async_computation.1 | async-start | bytes 25165824 | tf_op jit(solution)/shard_map/all_to_all | solution.py:70
  747.7 6.5 copy-start.1
  747.7 100.0 %all-to-all-start.3 = ((bf16[2048,16,128]{2,1,0:T(8,128)(2,1)}), bf16[2048,16,128]{2,1,0:T(8,128)(2,1)}, u32[]{:S(2)}, u32[]{:S(2)}) async-start(bf16[2048,16,128]{2,1,0:T(8,128)(2,1)} %bitcast.60), calls=%async_computation.3 | async-start | bytes 16777216 | tf_op jit(solution)/shard_map/all_to_all | solution.py:84
where the time goes:
time: 954 us; the launch traced here: 939 us
  matrix products  467 us (49%)
  waiting for transfers between devices  308 us (32%)
  local copies, waits for them, and re-layouts  106 us (11%)
  other arithmetic  26.9 us (3%)
  starting transfers between devices  25.2 us (3%)
    sub x8, matrix products, block_attention(): attn_prob = jax.nn.softmax(logits, axis=-1).astype(jnp.bfloat16)  159 us
    dot_general x8, matrix products, block_attention(): jnp.einsum('hqk,khv->qhv', attn_prob, v_heads, preferred_element_type=jnp...  124 us
    all_to_all x1, waiting for transfers between devices, local_step(): k_heads = lax.all_to_all(k_all, 'sp', 1, 0, tiled=True)  120 us
    all_to_all x1, waiting for transfers between devices, local_step(): q_heads = lax.all_to_all(q_all, 'sp', 1, 0, tiled=True)  94.9 us
    all_to_all x1, waiting for transfers between devices, local_step(): o_local = lax.all_to_all(o_heads, 'sp', 0, 1, tiled=True)  92.6 us
    dot_general x1, matrix products, local_step(): jnp.einsum('thv,hvd->td', o_local, w_o, preferred_element_type=jnp.float32)  81.9 us
    dot_general x1, matrix products, local_step(): jnp.einsum('tc,che->the', q_lat, w_uq, preferred_element_type=jnp.float32)  54.3 us
    unnamed x16, local copies, waits for them, and re-layouts  25.8 us
  transfers between devices with their start and end apart: 4, of which 3 were waited for; matrix products, arithmetic and copies ran while one was open for 18% of the time, Pallas kernels for 0%

commit v1 on v0

v1 whole, which is shorter than its diff:
```python
import functools
import math
import jax
import jax.numpy as jnp
from jax import lax
from jax.experimental import pallas as pl
from jax.experimental.pallas import tpu as pltpu
from jax.sharding import PartitionSpec as P

ROPE_THETA = 10000.0
YARN_FACTOR = 40.0
ORIG_CTX = 4096.0
BETA_FAST = 32.0
BETA_SLOW = 1.0
NORM_EPS = 1e-6
MESH = pl.DeviceIdType.MESH
LANES = 128
NEG = -1e30
GROUP = 4


def rope_freqs(rot_dim):
    half_dim = rot_dim // 2
    log_base = 2.0 * math.log(ROPE_THETA)
    low_idx = max(math.floor(rot_dim * math.log(ORIG_CTX / (BETA_FAST * 2.0 * math.pi)) / log_base), 0)
    high_idx = min(math.ceil(rot_dim * math.log(ORIG_CTX / (BETA_SLOW * 2.0 * math.pi)) / log_base), half_dim - 1)
    spread = max(high_idx - low_idx, 0.001)
    freq_list = []
    for freq_idx in range(half_dim):
        base_freq = ROPE_THETA ** (-2.0 * freq_idx / rot_dim)
        ramp_val = min(max((freq_idx - low_idx) / spread, 0.0), 1.0)
        freq_list.append(base_freq / YARN_FACTOR * ramp_val + base_freq * (1.0 - ramp_val))
    return jnp.asarray(freq_list, dtype=jnp.float32)


def rotate_half(act_in, cos_t, sin_t):
    half_dim = act_in.shape[-1] // 2
    first = act_in[..., :half_dim]
    second = act_in[..., half_dim:]
    return jnp.concatenate([first * cos_t - second * sin_t, second * cos_t + first * sin_t], axis=-1)


def rms_norm(act_in, gain):
    mean_sq = jnp.mean(act_in * act_in, axis=-1, keepdims=True)
    return act_in * lax.rsqrt(mean_sq + NORM_EPS) * gain


def dot_nt(a, b):
    return lax.dot_general(a, b, (((1,), (1,)), ((), ())), preferred_element_type=jnp.float32)


def dot_nn(a, b):
    return jnp.dot(a, b, preferred_element_type=jnp.float32)


SUB = 16
CBLK = 64


def gather_kernel(n, heads, nope, kv_ref, cq_ref, wt_ref, sel_ref, kv_all, cq_all, wn_ref, wr_ref, tn, tr, send_sem, recv_sem, loc_sem):
    step = pl.program_id(0)
    last = pl.num_programs(0) - 1
    me = lax.axis_index("sp")
    right = lax.rem(me + 2, n)
    left = lax.rem(me + n - 2, n)
    mate = me + 1 - 2 * lax.rem(me, 2)
    rows = kv_ref.shape[0]
    half = rows // 2
    srcs = (kv_ref, cq_ref)
    alls = (kv_all, cq_all)

    def piece(arr, owner, off, size):
        return alls[arr].at[pl.ds(pl.multiple_of(owner * rows + off, half), size)]

    def rcopy(arr, idx, src, owner, off, size, dev):
        return pltpu.make_async_remote_copy(
            src_ref=src, dst_ref=piece(arr, owner, off, size),
            send_sem=send_sem.at[arr, idx], recv_sem=recv_sem.at[arr, idx],
            device_id={"sp": dev}, device_id_type=MESH)

    def copies(arr):
        own = srcs[arr]
        opp = lax.rem(me + 4, n)
        c = {}
        c[0] = rcopy(arr, 0, own.at[pl.ds(0, half)], me, 0, half, right)
        c[1] = rcopy(arr, 1, own.at[pl.ds(half, half)], me, half, half, right)
        c[2] = rcopy(arr, 2, own.at[pl.ds(half, half)], me, half, half, left)
        c[3] = rcopy(arr, 3, own.at[pl.ds(0, half)], me, 0, half, left)
        c[4] = rcopy(arr, 4, own, me, 0, rows, mate)
        c[5] = rcopy(arr, 5, piece(arr, left, 0, half), left, 0, half, right)
        c[6] = rcopy(arr, 6, piece(arr, right, half, half), right, half, half, left)
        c[7] = rcopy(arr, 7, piece(arr, left, 0, rows), left, 0, rows, mate)
        c[8] = rcopy(arr, 8, piece(arr, right, 0, rows), right, 0, rows, mate)
        c[9] = rcopy(arr, 9, piece(arr, opp, 0, half), opp, 0, half, mate)
        c[10] = rcopy(arr, 10, piece(arr, opp, half, half), opp, half, half, mate)
        return c

    ckv = copies(0)
    ccq = copies(1)

    def local(arr):
        return pltpu.make_async_copy(srcs[arr], piece(arr, me, 0, rows), loc_sem.at[arr])

    @pl.when(step == 0)
    def _():
        barrier = pltpu.get_barrier_semaphore()
        for dev in (left, right, mate):
            pl.semaphore_signal(barrier, inc=1, device_id={"sp": dev}, device_id_type=MESH)
        pl.semaphore_wait(barrier, 3)
        for c in (ckv, ccq):
            for i in (0, 2, 1, 3, 4):
                c[i].start()
        for arr in range(2):
            local(arr).start()

    @pl.when(step == last // 4)
    def _():
        ckv[0].wait_recv()
        ckv[5].start()
        ckv[2].wait_recv()
        ckv[6].start()

    @pl.when(step == last // 2)
    def _():
        ckv[1].wait_recv()
        ckv[7].start()
        ckv[3].wait_recv()
        ckv[8].start()

    @pl.when(step == (3 * last) // 4)
    def _():
        ccq[0].wait_recv()
        ccq[5].start()
        ccq[2].wait_recv()
        ccq[6].start()

    for s in range(CBLK // SUB):
        lhs = jnp.concatenate([wt_ref[s * SUB + i] for i in range(SUB)], axis=1)
        g = dot_nn(lhs, sel_ref[...])
        width = g.shape[1] // 2
        tn[s] = g[:nope].T
        tr[s] = jnp.concatenate([g[nope:, :width], g[nope:, width:]], axis=0).T
        pairs = heads // 2
        for h in range(heads):
            par, hp = h % 2, h // 2
            wn_ref[s * SUB:(s + 1) * SUB, h * nope:(h + 1) * nope] = tn[s, pl.ds(par * width + hp, SUB, stride=pairs), :].astype(jnp.bfloat16)
        for hp in range(pairs):
            wr_ref[s * SUB:(s + 1) * SUB, hp * LANES:(hp + 1) * LANES] = tr[s, pl.ds(hp, SUB, stride=pairs), :].astype(jnp.bfloat16)

    @pl.when(step == last)
    def _():
        ccq[1].wait_recv()
        ccq[7].start()
        ccq[3].wait_recv()
        ccq[8].start()
        for c in (ckv, ccq):
            c[5].wait_recv()
            c[9].start()
            c[6].wait_recv()
            c[10].start()
        for c in (ckv, ccq):
            for i in (4, 7, 8, 9, 10):
                c[i].wait_recv()
            for i in range(11):
                c[i].wait_send()
        for arr in range(2):
            local(arr).wait()


def gather_and_pick(n, heads, nope, kv_own, cq_own, w_t, sel):
    rows, kvw = kv_own.shape
    rank = cq_own.shape[1]
    qk = w_t.shape[1]
    bf = jnp.bfloat16
    return pl.pallas_call(
        functools.partial(gather_kernel, n, heads, nope),
        grid=(rank // CBLK,),
        in_specs=[
            pl.BlockSpec((rows, kvw), lambda s: (0, 0)),
            pl.BlockSpec((rows, rank), lambda s: (0, 0)),
            pl.BlockSpec((CBLK, qk, w_t.shape[2]), lambda s: (s, 0, 0)),
            pl.BlockSpec(sel.shape, lambda s: (0, 0)),
        ],
        out_specs=[
            pl.BlockSpec(memory_space=pl.ANY),
            pl.BlockSpec(memory_space=pl.ANY),
            pl.BlockSpec((CBLK, heads * nope), lambda s: (s, 0)),
            pl.BlockSpec((CBLK, heads * (qk - nope)), lambda s: (s, 0)),
        ],
        out_shape=[
            jax.ShapeDtypeStruct((n * rows, kvw), bf),
            jax.ShapeDtypeStruct((n * rows, rank), bf),
            jax.ShapeDtypeStruct((rank, heads * nope), bf),
            jax.ShapeDtypeStruct((rank, heads * (qk - nope)), bf),
        ],
        scratch_shapes=[
            pltpu.VMEM((CBLK // SUB, SUB * heads, nope), jnp.float32),
            pltpu.VMEM((CBLK // SUB, SUB * heads // 2, LANES), jnp.float32),
            pltpu.SemaphoreType.DMA((2, 11)),
            pltpu.SemaphoreType.DMA((2, 11)),
            pltpu.SemaphoreType.DMA((2,)),
        ],
        compiler_params=pltpu.CompilerParams(collective_id=0, has_side_effects=True, dimension_semantics=("arbitrary",)),
        cost_estimate=pl.CostEstimate(flops=30_000_000_000, bytes_accessed=90_000_000, transcendentals=0),
        name="gather_pick",
    )(kv_own, cq_own, w_t, sel)


QB = 512


def attn_kernel(scale2, kv_rank, nope, rot, kv_ref, cq_ref, cos_ref, sin_ref, wn_ref, wr_ref, uk_ref, uvt_ref, o_ref, kcat, vt, qcat, acc, mrow, lrow):
    b = pl.program_id(0)
    vd = uvt_ref.shape[0] // GROUP
    bf = jnp.bfloat16

    @pl.when(b == 0)
    def _():
        def fill(i, _):
            r = pl.ds(pl.multiple_of(i * QB, QB), QB)
            c = kv_ref[r, :kv_rank]
            k = dot_nn(c, uk_ref[...]).astype(bf)
            raw = kv_ref[r, kv_rank:kv_rank + LANES].astype(jnp.float32)
            lane = lax.broadcasted_iota(jnp.int32, raw.shape, 1)
            pe_f = jnp.where(lane < rot, raw, 0.0)
            pe = (pe_f.astype(bf), pltpu.roll(pe_f, rot, 1).astype(bf))
            for h in range(GROUP):
                kcat[h, r, :nope] = k[:, h * nope:(h + 1) * nope]
                kcat[h, r, nope:] = pe[h % 2]
            vt[:, r] = dot_nt(uvt_ref[...], c).astype(bf)
            return 0
        lax.fori_loop(0, kv_ref.shape[0] // QB, fill, 0)

    cq = cq_ref[...]
    qn = dot_nn(cq, wn_ref[...]).astype(bf)
    qr = dot_nn(cq, wr_ref[...])
    cos_t = cos_ref[...]
    sin_t = sin_ref[...]
    for pr in range(GROUP // 2):
        z = qr[:, pr * LANES:(pr + 1) * LANES]
        lane = lax.broadcasted_iota(jnp.int32, z.shape, 1)
        hd = rot // 2
        swapped = jnp.where((lane // hd) % 2 == 0, pltpu.roll(z, LANES - hd, 1), pltpu.roll(z, hd, 1))
        zr = (z * cos_t + swapped * sin_t).astype(bf)
        for m in range(2):
            h = 2 * pr + m
            qcat[h, :, :nope] = qn[:, h * nope:(h + 1) * nope]
            qcat[h, :, nope:] = zr

    hb = QB // 2
    r0 = pl.multiple_of(b * QB, QB)
    tri = lax.broadcasted_iota(jnp.int32, (hb, hb), 0) <= lax.broadcasted_iota(jnp.int32, (hb, hb), 1)
    for h in range(GROUP):
        vrow = slice(h * vd, (h + 1) * vd)
        q0 = qcat[h, :hb, :]
        q1 = qcat[h, hb:, :]
        k0 = kcat[h, pl.ds(r0, hb), :]
        s00 = jnp.where(tri, dot_nt(k0, q0), NEG)
        m0 = jnp.max(s00, axis=0, keepdims=True)
        p00 = jnp.exp2((s00 - m0) * scale2)
        l0 = jnp.sum(p00, axis=0, keepdims=True)
        acc[h, :, :hb] = dot_nn(vt[vrow, pl.ds(r0, hb)], p00.astype(bf))
        k01 = kcat[h, pl.ds(r0, QB), :]
        s1 = dot_nt(k01, q1)
        s10 = s1[:hb]
        s11 = jnp.where(tri, s1[hb:], NEG)
        m1 = jnp.maximum(jnp.max(s10, axis=0, keepdims=True), jnp.max(s11, axis=0, keepdims=True))
        p10 = jnp.exp2((s10 - m1) * scale2)
        p11 = jnp.exp2((s11 - m1) * scale2)
        l1 = jnp.sum(p10, axis=0, keepdims=True) + jnp.sum(p11, axis=0, keepdims=True)
        p1 = jnp.concatenate([p10.astype(bf), p11.astype(bf)], axis=0)
        acc[h, :, hb:] = dot_nn(vt[vrow, pl.ds(r0, QB)], p1)
        mrow[h, :, :hb] = m0
        mrow[h, :, hb:] = m1
        lrow[h, :, :hb] = l0
        lrow[h, :, hb:] = l1

    def body(kb, _):
        r = pl.multiple_of(kb * QB, QB)
        for h in range(GROUP):
            vrow = slice(h * vd, (h + 1) * vd)
            s = dot_nt(kcat[h, pl.ds(r, QB), :], qcat[h])
            m_old = mrow[h]
            m_new = jnp.maximum(m_old, jnp.max(s, axis=0, keepdims=True))
            p = jnp.exp2((s - m_new) * scale2)
            alpha = jnp.exp2((m_old - m_new) * scale2)
            mrow[h] = m_new
            lrow[h] = lrow[h] * alpha + jnp.sum(p, axis=0, keepdims=True)
            acc[h] = acc[h] * alpha + dot_nn(vt[vrow, pl.ds(r, QB)], p.astype(bf))
        return 0

    lax.fori_loop(0, b, body, 0)

    for h in range(GROUP):
        o_ref[:, h * vd:(h + 1) * vd] = (acc[h] / lrow[h]).T.astype(bf)


def attention_group(g, scale2, kv_rank, nope, rot, vd, kv_all, cq_all, cos2, sin2, wn, wr, uk, uvt):
    seq, rank = cq_all.shape
    bf = jnp.bfloat16
    f32 = jnp.float32
    pairs = seq * (seq + QB) // 2
    flops = 2 * GROUP * (seq * rank * (nope + rot) + seq * kv_rank * (nope + vd) + pairs * (nope + rot + vd) * 2)
    return pl.pallas_call(
        functools.partial(attn_kernel, scale2, kv_rank, nope, rot),
        grid=(seq // QB,),
        in_specs=[
            pl.BlockSpec(kv_all.shape, lambda b: (0, 0)),
            pl.BlockSpec((QB, rank), lambda b: (b, 0)),
            pl.BlockSpec((QB, LANES), lambda b: (b, 0)),
            pl.BlockSpec((QB, LANES), lambda b: (b, 0)),
            pl.BlockSpec((rank, GROUP * nope), lambda b: (0, g)),
            pl.BlockSpec((rank, GROUP * rot), lambda b: (0, g)),
            pl.BlockSpec((kv_rank, GROUP * nope), lambda b: (0, g)),
            pl.BlockSpec((GROUP * vd, kv_rank), lambda b: (g, 0)),
        ],
        out_specs=pl.BlockSpec((QB, GROUP * vd), lambda b: (b, 0)),
        out_shape=jax.ShapeDtypeStruct((seq, GROUP * vd), bf),
        scratch_shapes=[
            pltpu.VMEM((GROUP, seq, nope + LANES), bf),
            pltpu.VMEM((GROUP * vd, seq), bf),
            pltpu.VMEM((GROUP, QB, nope + LANES), bf),
            pltpu.VMEM((GROUP, vd, QB), f32),
            pltpu.VMEM((GROUP, 1, QB), f32),
            pltpu.VMEM((GROUP, 1, QB), f32),
        ],
        compiler_params=pltpu.CompilerParams(dimension_semantics=("arbitrary",), vmem_limit_bytes=60_000_000),
        cost_estimate=pl.CostEstimate(flops=flops, bytes_accessed=12_000_000, transcendentals=pairs * GROUP),
        name="mla_attn",
    )(kv_all, cq_all, cos2, sin2, wn, wr, uk, uvt)


def out_kernel(first, final, *refs):
    if first:
        o_ref, w_ref, out_ref = refs[:3]
    else:
        acc_in, o_ref, w_ref, out_ref = refs[:4]
    acc = refs[-1] if final else out_ref
    step = pl.program_id(0)
    hw = w_ref.shape[0] * w_ref.shape[1]
    n = w_ref.shape[2]
    tile = 1024
    for t in range(n // tile):
        cols = slice(t * tile, (t + 1) * tile)
        prod = dot_nn(o_ref[...], w_ref[:, :, cols].reshape(hw, tile))
        if first:
            @pl.when(step == 0)
            def _():
                acc[:, cols] = prod

            @pl.when(step > 0)
            def _():
                acc[:, cols] += prod
        else:
            @pl.when(step == 0)
            def _():
                acc[:, cols] = acc_in[:, cols] + prod

            @pl.when(step > 0)
            def _():
                acc[:, cols] += prod
    if final:
        @pl.when(step == pl.num_programs(0) - 1)
        def _():
            out_ref[...] = acc[...].astype(out_ref.dtype)


def out_product(acc, o, w_o, chunk0, chunks, per_dev, n, final):
    seq, width = o.shape
    rows = seq // n
    hidden = w_o.shape[2]
    hc = width // w_o.shape[1] // chunks
    first = acc is None
    blocks = per_dev // hc
    steps = n * chunks
    in_specs = [] if first else [pl.BlockSpec((rows, hidden), lambda s: (0, 0), pipeline_mode=pl.Buffered(buffer_count=1))]
    in_specs += [
        pl.BlockSpec((rows, hc * w_o.shape[1]), lambda s: (s // chunks, s % chunks)),
        pl.BlockSpec((hc, w_o.shape[1], hidden), lambda s: ((s // chunks) * blocks + chunk0 + s % chunks, 0, 0)),
    ]
    args = ([] if first else [acc]) + [o, w_o]
    return pl.pallas_call(
        functools.partial(out_kernel, first, final),
        grid=(steps,),
        in_specs=in_specs,
        out_specs=pl.BlockSpec((rows, hidden), lambda s: (0, 0)),
        out_shape=jax.ShapeDtypeStruct((rows, hidden), jnp.bfloat16 if final else jnp.float32),
        scratch_shapes=[pltpu.VMEM((rows, hidden), jnp.float32)] if final else [],
        compiler_params=pltpu.CompilerParams(dimension_semantics=("arbitrary",), vmem_limit_bytes=60_000_000),
        cost_estimate=pl.CostEstimate(flops=2 * rows * hidden * width * n, bytes_accessed=2 * hidden * width * n, transcendentals=0),
        name="out_product",
    )(*args)


def solution(mesh):
    n = mesh.shape['sp']
    rows_spec = P(('dp', 'sp'), None)
    tok_spec = P(('dp', 'sp'))
    rep = P()

    def local_step(tok_in, tok_pos, w_dq, g_q, w_uq, w_dkv, g_kv, w_uk, w_uv, w_o):
        bf = jnp.bfloat16
        f32 = jnp.float32
        rows = tok_in.shape[0]
        num_heads = w_uq.shape[1]
        heads = num_heads // n
        qk_dim = w_uq.shape[2]
        kv_rank = g_kv.shape[0]
        rot = w_dkv.shape[1] - kv_rank
        nope = qk_dim - rot
        vd = w_uv.shape[2]
        rank = g_q.shape[0]
        scale2 = (0.1 * math.log(YARN_FACTOR) + 1.0) ** 2 / math.sqrt(qk_dim) / math.log(2.0)
        me = lax.axis_index('sp')

        freqs = rope_freqs(rot)
        angles = tok_pos.astype(f32)[:, None] * freqs[None, :]
        kv_lat = jnp.dot(tok_in, w_dkv, preferred_element_type=f32)
        cache_kv = rms_norm(kv_lat[:, :kv_rank], g_kv).astype(bf)
        cache_pe = rotate_half(kv_lat[:, kv_rank:], jnp.cos(angles), jnp.sin(angles)).astype(bf)
        digits = jnp.stack([tok_pos // LANES, tok_pos % LANES], axis=1).astype(bf)
        kv_own = jnp.concatenate([cache_kv, cache_pe, digits, jnp.zeros((rows, LANES - rot - 2), bf)], axis=1)
        cq_own = rms_norm(jnp.dot(tok_in, w_dq, preferred_element_type=f32), g_q).astype(bf)

        ri = lax.broadcasted_iota(jnp.int32, (SUB * num_heads, SUB * heads), 0)
        ci = lax.broadcasted_iota(jnp.int32, (SUB * num_heads, SUB * heads), 1)
        width = SUB * heads // 2
        want_c = (ci % width) // (heads // 2)
        want_h = me * heads + 2 * (ci % (heads // 2)) + ci // width
        sel = ((ri // num_heads == want_c) & (ri % num_heads == want_h)).astype(bf)

        w_t = jnp.transpose(w_uq, (0, 2, 1))
        kv_all, cq_all, wn, wr = gather_and_pick(n, heads, nope, kv_own, cq_own, w_t, sel)

        uk = lax.dynamic_slice_in_dim(w_uk, me * heads, heads, axis=1).reshape(kv_rank, heads * nope)
        uvt = jnp.transpose(lax.dynamic_slice_in_dim(w_uv, me * heads, heads, axis=1), (1, 2, 0)).reshape(heads * vd, kv_rank)

        digs = kv_all[:, kv_rank + rot:kv_rank + rot + 2].astype(f32)
        ang = (digs[:, :1] * LANES + digs[:, 1:2]) * freqs[None, :]
        cos_a, sin_a = jnp.cos(ang), jnp.sin(ang)
        cos2 = jnp.concatenate([cos_a] * 4, axis=1)
        sin2 = jnp.concatenate([-sin_a, sin_a] * 2, axis=1)

        chunks = heads // GROUP
        o_parts = []
        for g in range(chunks):
            o_g = attention_group(g, scale2, kv_rank, nope, rot, vd, kv_all, cq_all, cos2, sin2, wn, wr, uk, uvt)
            o_parts.append(lax.all_to_all(o_g, 'sp', 0, 0, tiled=True))
        acc = None
        for g in range(chunks):
            acc = out_product(acc, o_parts[g], w_o, g, 1, heads, n, g == chunks - 1)
        return acc, cache_kv, cache_pe

    return jax.shard_map(local_step, mesh=mesh, in_specs=(rows_spec, tok_spec, rep, rep, rep, rep, rep, rep, rep, rep), out_specs=(rows_spec, rows_spec, rows_spec), check_vma=False)
```

time: 954 us -> 443 us (0.46)
  matrix products: 467 us -> 19.3 us
  Pallas kernels: 0 us -> 363 us
  waiting for transfers between devices: 308 us -> 0.01 us
  local copies, waits for them, and re-layouts: 106 us -> 15 us
  other arithmetic: 26.9 us -> 16.3 us
    pallas_call x0 -> x9, Pallas kernels: none -> 363 us  [the longest x4 160 us: attention_group(): pl.pallas_call(functools.partial(attn_kernel, scale2, kv_rank, nope, rot)...]
    all_to_all x4, waiting for transfers between devices: 308 us -> 0.01 us  [local_step(): o_parts.append(lax.all_to_all(o_g, 'sp', 0, 0, tiled=True))]
    dot_general x13 -> x2, matrix products: 299 us -> 19.3 us  [the longest x1 11.6 us: local_step(): jnp.dot(tok_in, w_dq, preferred_element_type=f32)]
    sub x8 -> x0, matrix products: 159 us -> none  [block_attention(): attn_prob = jax.nn.softmax(logits, axis=-1).astype(jnp.bfloat16)]
    all_to_all x4 -> x0, local copies, waits for them, and re-layouts: 38.3 us -> none  [the longest x1 10.8 us: local_step(): q_heads = lax.all_to_all(q_all, 'sp', 1, 0, tiled=True)]
    unnamed x16 -> x18, local copies, waits for them, and re-layouts: 25.8 us -> 5.28 us
    concatenate x1, local copies, waits for them, and re-layouts: 17 us -> 0.89 us  [local_step(): jnp.concatenate([cache_kv, cache_pe, digits, jnp.zeros((rows, LANES - rot...]
    concatenate x2, other arithmetic: 17.2 us -> 3.77 us  [the longest x1 1.92 us: local_step(): cos2 = jnp.concatenate([cos_a] * 4, axis=1)]
  transfers between devices with their start and end apart: 4 -> 4, of which waited for: 3 -> 0; matrix products, arithmetic and copies ran while one was open for 18% -> 0% of each run, Pallas kernels for 0% -> 54%
where the time goes in v1:
time: 443 us; the launch traced here: 434 us
  Pallas kernels  363 us (82%)
  matrix products  19.3 us (4%)
  starting transfers between devices  19.3 us (4%)
  other arithmetic  16.3 us (4%)
  local copies, waits for them, and re-layouts  15 us (3%)
    pallas_call x4, Pallas kernels, attention_group(): pl.pallas_call(functools.partial(attn_kernel, scale2, kv_rank, nope, rot)...  160 us
    pallas_call x4, Pallas kernels, out_product(): pl.pallas_call(functools.partial(out_kernel, first, final), grid=(steps,)...  151 us
    pallas_call x1, Pallas kernels, gather_and_pick(): pl.pallas_call(functools.partial(gather_kernel, n, heads, nope), grid=(ra...  52.3 us
    all_to_all x4, starting transfers between devices, local_step(): o_parts.append(lax.all_to_all(o_g, 'sp', 0, 0, tiled=True))  19.3 us
    dot_general x1, matrix products, local_step(): jnp.dot(tok_in, w_dq, preferred_element_type=f32)  11.6 us
  transfers between devices with their start and end apart: 4, of which 0 were waited for; matrix products, arithmetic and copies ran while one was open for 0% of the time, Pallas kernels for 54%

profile of v1, /device:TPU:81, one launch (start us, length us, event | category | flops | bytes accessed | tf_op | source)
XLA Modules:
  0.0 434.5 jit_solution(4356128026297710196)
XLA Ops:
  1.7 7.6 %fusion.29 = f32[256,576]{1,0:T(8,128)S(1)} fusion(bf16[256,7168]{1,0:T(8,128)(2,1)} %param.11, bf16[7168,576]{0,1:T(8,128)(2,1)} %param.16), kind=kOutput, calls=%fused_computation.75 | convolution fusion | flops 2113929216 | bytes 12517376 | tf_op jit(solution)/shard_map/dot_general | solution.py:418
  9.5 11.6 %multiply_reduce_fusion = (f32[256]{0:T(256)S(1)}, f32[256,1536]{1,0:T(8,128)}) fusion(bf16[256,7168]{1,0:T(8,128)(2,1)S(1)} %copy-done.7, bf16[7168,1536]{1,0:T(8,128)(2,1)} %param.13), kind=kOutput, calls=%fused_computation.19 | convolution fusion | flops 5637931008 | bytes 27264000 | tf_op jit(solution)/shard_map/dot_general | solution.py:423
  21.1 4.3 dynamic-slice_bitcast_fusion
  25.4 4.3 copy.33
  29.8 1.9 copy.38
  34.4 4.1 fusion.7.sel_ref
  38.6 52.3 %gather_pick.1 = (bf16[2048,640]{1,0:T(8,128)(2,1)}, bf16[2048,1536]{1,0:T(8,128)(2,1)}, bf16[1536,2048]{1,0:T(8,128)(2,1)}, bf16[1536,1024]{1,0:T(8,128)(2,1)}) custom-call(bf16[256,640]{1,0:T(8,128)(2,1)} %concatenate.14.kv_ref, bf16[256,1536]{1,0:T(8,128)(2,1)} %multiply_convert_fusion.cq_ref, bf16[1536,192,128]{2,1,0:T(8,128)(2,1)} %bitcast.wt_ref, ...), custom_call_target="tpu_custom_call" | custom-call | flops 30000001024 | bytes 90000000 | tf_op jit(solution)/shard_map/gather_pick/pallas_call | solution.py:175
  92.7 3.7 fusion.9
  96.4 1.9 pad_maximum_fusion.cos_ref
  98.4 1.9 pad_maximum_fusion.1.sin_ref
  100.2 40.0 %mla_attn.6 = bf16[2048,512]{1,0:T(8,128)(2,1)} custom-call(bf16[2048,640]{1,0:T(8,128)(2,1)} %get-tuple-element.7.kv_ref, bf16[2048,1536]{1,0:T(8,128)(2,1)} %get-tuple-element.8.cq_ref, f32[2048,128]{1,0:T(8,128)} %pad_maximum_fusion.cos_ref, f32[2048,128]{1,0:T(8,128)} %pad_maximum_fusion.1.sin_ref, bf16[1536,2048]{1,0:T(8,128)(2,1)} %get-tuple-element.9.wn_ref, ...), custom_call_target="tpu_custom_call" | custom-call | flops 20401094656 | bytes 12000000 | tf_op jit(solution)/shard_map/mla_attn/pallas_call | solution.py:304
  140.2 4.0 all-to-all-start.2
  144.2 40.2 %mla_attn.4 = bf16[2048,512]{1,0:T(8,128)(2,1)} custom-call(bf16[2048,640]{1,0:T(8,128)(2,1)} %get-tuple-element.7.kv_ref, bf16[2048,1536]{1,0:T(8,128)(2,1)} %get-tuple-element.8.cq_ref, f32[2048,128]{1,0:T(8,128)} %pad_maximum_fusion.cos_ref, f32[2048,128]{1,0:T(8,128)} %pad_maximum_fusion.1.sin_ref, bf16[1536,2048]{1,0:T(8,128)(2,1)} %get-tuple-element.9.wn_ref, ...), custom_call_target="tpu_custom_call" | custom-call | flops 20401094656 | bytes 12000000 | tf_op jit(solution)/shard_map/mla_attn/pallas_call | solution.py:304
  184.4 1.4 copy-done
  185.8 4.9 %all-to-all-start = ((bf16[8,256,512]{2,1,0:T(8,128)(2,1)}), bf16[8,256,512]{2,1,0:T(8,128)(2,1)}, u32[]{:S(2)}, u32[]{:S(2)}) async-start(bf16[8,256,512]{2,1,0:T(8,128)(2,1)} %bitcast.33), calls=%async_computation | async-start | bytes 4194304 | tf_op jit(solution)/shard_map/all_to_all | solution.py:448
  190.7 40.0 %mla_attn.5 = bf16[2048,512]{1,0:T(8,128)(2,1)} custom-call(bf16[2048,640]{1,0:T(8,128)(2,1)} %get-tuple-element.7.kv_ref, bf16[2048,1536]{1,0:T(8,128)(2,1)} %get-tuple-element.8.cq_ref, f32[2048,128]{1,0:T(8,128)} %pad_maximum_fusion.cos_ref, f32[2048,128]{1,0:T(8,128)} %pad_maximum_fusion.1.sin_ref, bf16[1536,2048]{1,0:T(8,128)(2,1)} %get-tuple-element.9.wn_ref, ...), custom_call_target="tpu_custom_call" | custom-call | flops 20401094656 | bytes 12000000 | tf_op jit(solution)/shard_map/mla_attn/pallas_call | solution.py:304
  230.6 5.2 %all-to-all-start.1 = ((bf16[8,256,512]{2,1,0:T(8,128)(2,1)}), bf16[8,256,512]{2,1,0:T(8,128)(2,1)S(1)}, u32[]{:S(2)}, u32[]{:S(2)}) async-start(bf16[8,256,512]{2,1,0:T(8,128)(2,1)} %bitcast.32), calls=%async_computation.1 | async-start | bytes 4194304 | tf_op jit(solution)/shard_map/all_to_all | solution.py:448
  235.8 40.0 %mla_attn.7 = bf16[2048,512]{1,0:T(8,128)(2,1)} custom-call(bf16[2048,640]{1,0:T(8,128)(2,1)} %get-tuple-element.7.kv_ref, bf16[2048,1536]{1,0:T(8,128)(2,1)} %get-tuple-element.8.cq_ref, f32[2048,128]{1,0:T(8,128)} %pad_maximum_fusion.cos_ref, f32[2048,128]{1,0:T(8,128)} %pad_maximum_fusion.1.sin_ref, bf16[1536,2048]{1,0:T(8,128)(2,1)} %get-tuple-element.9.wn_ref, ...), custom_call_target="tpu_custom_call" | custom-call | flops 20401094656 | bytes 12000000 | tf_op jit(solution)/shard_map/mla_attn/pallas_call | solution.py:304
  276.7 35.9 %out_product.4.refs_0_ = f32[256,7168]{1,0:T(8,128)} custom-call(bf16[2048,512]{1,0:T(8,128)(2,1)} %bitcast.4.refs_0_, bf16[128,128,7168]{2,1,0:T(8,128)(2,1)} %refs_2_.5), custom_call_target="tpu_custom_call" | custom-call | flops 15032385536 | bytes 58720256 | tf_op jit(solution)/shard_map/out_product/pallas_call | solution.py:382
  312.6 1.3 copy-done.1
  313.9 5.2 %all-to-all-start.3 = ((bf16[8,256,512]{2,1,0:T(8,128)(2,1)}), bf16[8,256,512]{2,1,0:T(8,128)(2,1)}, u32[]{:S(2)}, u32[]{:S(2)}) async-start(bf16[8,256,512]{2,1,0:T(8,128)(2,1)} %bitcast.31), calls=%async_computation.3 | async-start | bytes 4194304 | tf_op jit(solution)/shard_map/all_to_all | solution.py:448
  319.1 38.6 %out_product.5.refs_0_ = f32[256,7168]{1,0:T(8,128)} custom-call(f32[256,7168]{1,0:T(8,128)} %out_product.4.refs_0_, bf16[2048,512]{1,0:T(8,128)(2,1)} %bitcast.21, bf16[128,128,7168]{2,1,0:T(8,128)(2,1)} %refs_2_.5), custom_call_target="tpu_custom_call" | custom-call | flops 15032385536 | bytes 58720256 | tf_op jit(solution)/shard_map/out_product/pallas_call | solution.py:382
  357.7 38.5 %out_product.6.refs_0_ = f32[256,7168]{1,0:T(8,128)} custom-call(f32[256,7168]{1,0:T(8,128)} %out_product.5.refs_0_, bf16[2048,512]{1,0:T(8,128)(2,1)} %bitcast.20, bf16[128,128,7168]{2,1,0:T(8,128)(2,1)} %refs_2_.5), custom_call_target="tpu_custom_call" | custom-call | flops 15032385536 | bytes 58720256 | tf_op jit(solution)/shard_map/out_product/pallas_call | solution.py:382
  396.3 37.8 %out_product.7 = bf16[256,7168]{1,0:T(8,128)(2,1)} custom-call(f32[256,7168]{1,0:T(8,128)} %out_product.6.refs_0_, bf16[2048,512]{1,0:T(8,128)(2,1)} %bitcast.10.refs_1_, bf16[128,128,7168]{2,1,0:T(8,128)(2,1)} %refs_2_.5), custom_call_target="tpu_custom_call" | custom-call | flops 15032385536 | bytes 58720256 | tf_op jit(solution)/shard_map/out_product/pallas_call | solution.py:382
  (41 shorter events, 6.5 us)
Async XLA Ops:
  1.7 7.8 %copy-start.7 = (bf16[256,7168]{1,0:T(8,128)(2,1)S(1)}, bf16[256,7168]{1,0:T(8,128)(2,1)}, u32[]{:S(2)}) copy-start(bf16[256,7168]{1,0:T(8,128)(2,1)} %param.11) | copy-start | bytes 11010052
  29.8 1.9 copy-start.6
  29.8 2.5 copy-start.5
  29.8 2.6 copy-start.2
  29.8 2.6 copy-start.4
  32.4 6.2 %copy-start.3 = (bf16[256,512]{1,0:T(8,128)(2,1)}, bf16[256,512]{1,0:T(8,128)(2,1)S(1)}, u32[]{:S(2)}) copy-start(bf16[256,512]{1,0:T(8,128)(2,1)S(1)} %multiply_convert_fusion.1) | copy-start | bytes 786436
  140.2 44.2 %all-to-all-start.2 = ((bf16[8,256,512]{2,1,0:T(8,128)(2,1)}), bf16[8,256,512]{2,1,0:T(8,128)(2,1)S(1)}, u32[]{:S(2)}, u32[]{:S(2)}) async-start(bf16[8,256,512]{2,1,0:T(8,128)(2,1)} %bitcast.34), calls=%async_computation.2 | async-start | bytes 4194304 | tf_op jit(solution)/shard_map/all_to_all | solution.py:448
  184.4 1.4 copy-start
  185.8 44.9 %all-to-all-start = ((bf16[8,256,512]{2,1,0:T(8,128)(2,1)}), bf16[8,256,512]{2,1,0:T(8,128)(2,1)}, u32[]{:S(2)}, u32[]{:S(2)}) async-start(bf16[8,256,512]{2,1,0:T(8,128)(2,1)} %bitcast.33), calls=%async_computation | async-start | bytes 4194304 | tf_op jit(solution)/shard_map/all_to_all | solution.py:448
  230.6 81.9 %all-to-all-start.1 = ((bf16[8,256,512]{2,1,0:T(8,128)(2,1)}), bf16[8,256,512]{2,1,0:T(8,128)(2,1)S(1)}, u32[]{:S(2)}, u32[]{:S(2)}) async-start(bf16[8,256,512]{2,1,0:T(8,128)(2,1)} %bitcast.32), calls=%async_computation.1 | async-start | bytes 4194304 | tf_op jit(solution)/shard_map/all_to_all | solution.py:448
  312.6 1.3 copy-start.1
  313.9 82.4 %all-to-all-start.3 = ((bf16[8,256,512]{2,1,0:T(8,128)(2,1)}), bf16[8,256,512]{2,1,0:T(8,128)(2,1)}, u32[]{:S(2)}, u32[]{:S(2)}) async-start(bf16[8,256,512]{2,1,0:T(8,128)(2,1)} %bitcast.31), calls=%async_computation.3 | async-start | bytes 4194304 | tf_op jit(solution)/shard_map/all_to_all | solution.py:448

commit v2 on v0

v2 whole, which is shorter than its diff:
```python
import functools
import math
import jax
import jax.numpy as jnp
from jax import lax
from jax.experimental import pallas as pl
from jax.experimental.pallas import tpu as pltpu
from jax.sharding import PartitionSpec as P

ROPE_THETA = 10000.0
YARN_FACTOR = 40.0
ORIG_CTX = 4096.0
BETA_FAST = 32.0
BETA_SLOW = 1.0
NORM_EPS = 1e-6
MESH = pl.DeviceIdType.MESH
LANES = 128
NEG = -1e30
GROUP = 4


def rope_freqs(rot_dim):
    half_dim = rot_dim // 2
    log_base = 2.0 * math.log(ROPE_THETA)
    low_idx = max(math.floor(rot_dim * math.log(ORIG_CTX / (BETA_FAST * 2.0 * math.pi)) / log_base), 0)
    high_idx = min(math.ceil(rot_dim * math.log(ORIG_CTX / (BETA_SLOW * 2.0 * math.pi)) / log_base), half_dim - 1)
    spread = max(high_idx - low_idx, 0.001)
    freq_list = []
    for freq_idx in range(half_dim):
        base_freq = ROPE_THETA ** (-2.0 * freq_idx / rot_dim)
        ramp_val = min(max((freq_idx - low_idx) / spread, 0.0), 1.0)
        freq_list.append(base_freq / YARN_FACTOR * ramp_val + base_freq * (1.0 - ramp_val))
    return jnp.asarray(freq_list, dtype=jnp.float32)


def rotate_half(act_in, cos_t, sin_t):
    half_dim = act_in.shape[-1] // 2
    first = act_in[..., :half_dim]
    second = act_in[..., half_dim:]
    return jnp.concatenate([first * cos_t - second * sin_t, second * cos_t + first * sin_t], axis=-1)


def rms_norm(act_in, gain):
    mean_sq = jnp.mean(act_in * act_in, axis=-1, keepdims=True)
    return act_in * lax.rsqrt(mean_sq + NORM_EPS) * gain


def dot_nt(a, b):
    return lax.dot_general(a, b, (((1,), (1,)), ((), ())), preferred_element_type=jnp.float32)


def dot_nn(a, b):
    return jnp.dot(a, b, preferred_element_type=jnp.float32)


def latent_kernel(kv_rank, x_ref, wq_ref, wkvt_ref, gq_ref, gkv_ref, cos_ref, sin_ref, cq_ref, kv_ref, pe_ref, own_ref, acc_q, acc_kv):
    step = pl.program_id(0)
    bf = jnp.bfloat16

    @pl.when(step == 0)
    def _():
        acc_q[...] = jnp.zeros_like(acc_q)
        acc_kv[...] = jnp.zeros_like(acc_kv)

    acc_q[...] += dot_nn(x_ref[...], wq_ref[...])
    acc_kv[...] += dot_nt(x_ref[...], wkvt_ref[...])

    @pl.when(step == pl.num_programs(0) - 1)
    def _():
        cq_ref[...] = rms_norm(acc_q[...], gq_ref[...]).astype(bf)
        lat = rms_norm(acc_kv[:, :kv_rank], gkv_ref[...]).astype(bf)
        kv_ref[...] = lat
        pe = rotate_half(acc_kv[:, kv_rank:], cos_ref[...], sin_ref[...]).astype(bf)
        pe_ref[...] = pe
        own_ref[:, :kv_rank] = lat
        own_ref[:, kv_rank:] = jnp.concatenate([pe, jnp.zeros((pe.shape[0], LANES - pe.shape[1]), bf)], axis=1)


def latents(x, w_dq, w_dkv, g_q, g_kv, cos_t, sin_t):
    rows, hidden = x.shape
    rank = w_dq.shape[1]
    kvw = w_dkv.shape[1]
    kv_rank = g_kv.shape[0]
    rot = kvw - kv_rank
    half = rot // 2
    kb = 512
    bf = jnp.bfloat16
    const = lambda s: (0, 0)
    return pl.pallas_call(
        functools.partial(latent_kernel, kv_rank),
        grid=(hidden // kb,),
        in_specs=[
            pl.BlockSpec((rows, kb), lambda s: (0, s)),
            pl.BlockSpec((kb, rank), lambda s: (s, 0)),
            pl.BlockSpec((kvw, kb), lambda s: (0, s)),
            pl.BlockSpec((1, rank), const),
            pl.BlockSpec((1, kv_rank), const),
            pl.BlockSpec((rows, half), const),
            pl.BlockSpec((rows, half), const),
        ],
        out_specs=[
            pl.BlockSpec((rows, rank), const),
            pl.BlockSpec((rows, kv_rank), const),
            pl.BlockSpec((rows, rot), const),
            pl.BlockSpec((rows, kv_rank + LANES), const),
        ],
        out_shape=[
            jax.ShapeDtypeStruct((rows, rank), bf),
            jax.ShapeDtypeStruct((rows, kv_rank), bf),
            jax.ShapeDtypeStruct((rows, rot), bf),
            jax.ShapeDtypeStruct((rows, kv_rank + LANES), bf),
        ],
        scratch_shapes=[pltpu.VMEM((rows, rank), jnp.float32), pltpu.VMEM((rows, kvw), jnp.float32)],
        compiler_params=pltpu.CompilerParams(dimension_semantics=("arbitrary",)),
        cost_estimate=pl.CostEstimate(flops=2 * rows * hidden * (rank + kvw), bytes_accessed=2 * hidden * (rank + kvw + rows), transcendentals=0),
        name="latents",
    )(x, w_dq, w_dkv.T, g_q[None, :], g_kv[None, :], cos_t, sin_t)


SUB = 16
CBLK = 96


def gather_kernel(n, heads, nope, kv_ref, cs_ref, cq_ref, wt_ref, uk_ref, uv_ref, kv_all, cs_all, cq_all, wn_ref, wr_ref, uko_ref, uvo_ref, sel, tn, tr, tu, send_sem, recv_sem, loc_sem):
    step = pl.program_id(0)
    last = pl.num_programs(0) - 1
    me = lax.axis_index("sp")
    right = lax.rem(me + 2, n)
    left = lax.rem(me + n - 2, n)
    mate = me + 1 - 2 * lax.rem(me, 2)
    opp = lax.rem(me + 4, n)
    srcs = (kv_ref, cs_ref, cq_ref)
    alls = (kv_all, cs_all, cq_all)
    num = len(srcs)
    bf = jnp.bfloat16

    def piece(arr, owner, part):
        rows = srcs[arr].shape[0]
        half = rows // 2
        off, size = ((0, half), (half, half), (0, rows))[part]
        return alls[arr].at[pl.ds(pl.multiple_of(owner * rows + off, half), size)]

    def own(arr, part):
        half = srcs[arr].shape[0] // 2
        return srcs[arr].at[pl.ds(0, half)] if part == 0 else srcs[arr].at[pl.ds(half, half)] if part == 1 else srcs[arr]

    def rcopy(arr, idx, src, owner, part, dev):
        return pltpu.make_async_remote_copy(
            src_ref=src, dst_ref=piece(arr, owner, part),
            send_sem=send_sem.at[arr, idx], recv_sem=recv_sem.at[arr, idx],
            device_id={"sp": dev}, device_id_type=MESH)

    def copies(arr):
        return [
            rcopy(arr, 0, own(arr, 0), me, 0, right),
            rcopy(arr, 1, own(arr, 1), me, 1, right),
            rcopy(arr, 2, own(arr, 1), me, 1, left),
            rcopy(arr, 3, own(arr, 0), me, 0, left),
            rcopy(arr, 4, own(arr, 2), me, 2, mate),
            rcopy(arr, 5, piece(arr, left, 0), left, 0, right),
            rcopy(arr, 6, piece(arr, right, 1), right, 1, left),
            rcopy(arr, 7, piece(arr, left, 2), left, 2, mate),
            rcopy(arr, 8, piece(arr, right, 2), right, 2, mate),
            rcopy(arr, 9, piece(arr, opp, 0), opp, 0, mate),
            rcopy(arr, 10, piece(arr, opp, 1), opp, 1, mate),
        ]

    cps = [copies(arr) for arr in range(num)]
    loc = [pltpu.make_async_copy(srcs[arr], piece(arr, me, 2), loc_sem.at[arr]) for arr in range(num)]
    width = SUB * heads // 2
    pairs = heads // 2
    lanes = wt_ref.shape[2]

    @pl.when(step == 0)
    def _():
        barrier = pltpu.get_barrier_semaphore()
        for dev in (left, right, mate):
            pl.semaphore_signal(barrier, inc=1, device_id={"sp": dev}, device_id_type=MESH)
        pl.semaphore_wait(barrier, 3)
        for arr in (2, 0, 1):
            for i in (0, 2, 1, 3, 4):
                cps[arr][i].start()
        for arr in range(num):
            loc[arr].start()
        hp = lax.broadcasted_iota(jnp.int32, (lanes, 2 * width), 0)
        col = lax.broadcasted_iota(jnp.int32, (lanes, 2 * width), 1)
        want_h = me * heads + 2 * lax.rem(col, pairs) + col // width
        want_c = lax.rem(col, width) // pairs
        code = jnp.where(hp == want_h, want_c, -1)
        for c in range(SUB):
            sel[c * lanes:(c + 1) * lanes, :] = jnp.where(code == c, 1.0, 0.0).astype(bf)

    @pl.when(step == last // 2)
    def _():
        cps[2][0].wait_recv()
        cps[2][5].start()
        cps[2][2].wait_recv()
        cps[2][6].start()

    for s in range(CBLK // SUB):
        lhs = jnp.concatenate([wt_ref[s * SUB + i] for i in range(SUB)], axis=1)
        g = dot_nn(lhs, sel[...])
        tn[s] = g[:nope].T
        tr[s] = jnp.concatenate([g[nope:, :width], g[nope:, width:]], axis=0).T
        for h in range(heads):
            par, hp = h % 2, h // 2
            wn_ref[s * SUB:(s + 1) * SUB, h * nope:(h + 1) * nope] = tn[s, pl.ds(par * width + hp, SUB, stride=pairs), :].astype(bf)
        for hp in range(pairs):
            wr_ref[s * SUB:(s + 1) * SUB, hp * LANES:(hp + 1) * LANES] = tr[s, pl.ds(hp, SUB, stride=pairs), :].astype(bf)

    cb = uk_ref.shape[0]
    for i, (src, dst) in enumerate(((uk_ref, uko_ref), (uv_ref, uvo_ref))):
        wd = src.shape[2]
        tu[i] = src[...].astype(jnp.float32).reshape(cb * heads, wd)
        for h in range(heads):
            dst[:, h * wd:(h + 1) * wd] = tu[i, pl.ds(h, cb, stride=heads), :].astype(bf)

    @pl.when(step == last)
    def _():
        cps[2][1].wait_recv()
        cps[2][7].start()
        cps[2][3].wait_recv()
        cps[2][8].start()
        for arr in (0, 1):
            cps[arr][0].wait_recv()
            cps[arr][5].start()
            cps[arr][2].wait_recv()
            cps[arr][6].start()
        for arr in (0, 1):
            cps[arr][1].wait_recv()
            cps[arr][7].start()
            cps[arr][3].wait_recv()
            cps[arr][8].start()
        for arr in (2, 0, 1):
            cps[arr][5].wait_recv()
            cps[arr][9].start()
            cps[arr][6].wait_recv()
            cps[arr][10].start()
        for arr in range(num):
            for i in (4, 7, 8, 9, 10):
                cps[arr][i].wait_recv()
            for i in range(11):
                cps[arr][i].wait_send()
            loc[arr].wait()


def gather_and_pick(n, heads, nope, kv_own, cs_own, cq_own, w_t, w_uk, w_uv):
    rank = cq_own.shape[1]
    qk = w_t.shape[1]
    kv_rank = w_uk.shape[0]
    vd = w_uv.shape[2]
    steps = rank // CBLK
    cb = kv_rank // steps
    bf = jnp.bfloat16
    f32 = jnp.float32
    const = lambda s: (0, 0)
    own_heads = lambda s: (s, lax.axis_index("sp"), 0)
    return pl.pallas_call(
        functools.partial(gather_kernel, n, heads, nope),
        grid=(steps,),
        in_specs=[
            pl.BlockSpec(kv_own.shape, const),
            pl.BlockSpec(cs_own.shape, const),
            pl.BlockSpec(cq_own.shape, const),
            pl.BlockSpec((CBLK, qk, w_t.shape[2]), lambda s: (s, 0, 0)),
            pl.BlockSpec((cb, heads, nope), own_heads),
            pl.BlockSpec((cb, heads, vd), own_heads),
        ],
        out_specs=[
            pl.BlockSpec(memory_space=pl.ANY),
            pl.BlockSpec(memory_space=pl.ANY),
            pl.BlockSpec(memory_space=pl.ANY),
            pl.BlockSpec((CBLK, heads * nope), lambda s: (s, 0)),
            pl.BlockSpec((CBLK, heads * (qk - nope)), lambda s: (s, 0)),
            pl.BlockSpec((cb, heads * nope), lambda s: (s, 0)),
            pl.BlockSpec((cb, heads * vd), lambda s: (s, 0)),
        ],
        out_shape=[
            jax.ShapeDtypeStruct((n * kv_own.shape[0], kv_own.shape[1]), bf),
            jax.ShapeDtypeStruct((n * cs_own.shape[0], cs_own.shape[1]), f32),
            jax.ShapeDtypeStruct((n * cq_own.shape[0], rank), bf),
            jax.ShapeDtypeStruct((rank, heads * nope), bf),
            jax.ShapeDtypeStruct((rank, heads * (qk - nope)), bf),
            jax.ShapeDtypeStruct((kv_rank, heads * nope), bf),
            jax.ShapeDtypeStruct((kv_rank, heads * vd), bf),
        ],
        scratch_shapes=[
            pltpu.VMEM((SUB * w_t.shape[2], SUB * heads), bf),
            pltpu.VMEM((CBLK // SUB, SUB * heads, nope), f32),
            pltpu.VMEM((CBLK // SUB, SUB * heads // 2, LANES), f32),
            pltpu.VMEM((2, cb * heads, nope), f32),
            pltpu.SemaphoreType.DMA((3, 11)),
            pltpu.SemaphoreType.DMA((3, 11)),
            pltpu.SemaphoreType.DMA((3,)),
        ],
        compiler_params=pltpu.CompilerParams(collective_id=0, has_side_effects=True, dimension_semantics=("arbitrary",), vmem_limit_bytes=60_000_000),
        cost_estimate=pl.CostEstimate(flops=30_000_000_000, bytes_accessed=90_000_000, transcendentals=0),
        name="gather_pick",
    )(kv_own, cs_own, cq_own, w_t, w_uk, w_uv)


QB = 512
CH = 16


def attn_kernel(scale2, kv_rank, nope, rot, kv_ref, cq_ref, cs_ref, wn_ref, wr_ref, uk_ref, uv_ref, o_ref, kcat, vt, uvt, qcat, acc, mrow, lrow, s0, s1, p0, p1, mx0, mx1, al0, al1):
    b = pl.program_id(0)
    vd = uv_ref.shape[1] // GROUP
    bf = jnp.bfloat16
    sbuf, pbuf, mxb, alb = (s0, s1), (p0, p1), (mx0, mx1), (al0, al1)
    hd = rot // 2
    hb = QB // 2

    @pl.when(b == 0)
    def _():
        uvt[...] = uv_ref[...].T

        def fill(i, _):
            r = pl.ds(pl.multiple_of(i * QB, QB), QB)
            c = kv_ref[r, :kv_rank]
            k = dot_nn(c, uk_ref[...]).astype(bf)
            pe_f = kv_ref[r, kv_rank:kv_rank + LANES].astype(jnp.float32)
            pe = (pe_f.astype(bf), pltpu.roll(pe_f, rot, 1).astype(bf))
            for h in range(GROUP):
                kcat[h, r, :nope] = k[:, h * nope:(h + 1) * nope]
                kcat[h, r, nope:] = pe[h % 2]
            vt[:, r] = dot_nt(uvt[...], c).astype(bf)
            return 0
        lax.fori_loop(0, kv_ref.shape[0] // QB, fill, 0)

    cq = cq_ref[...]
    qn = dot_nn(cq, wn_ref[...]).astype(bf)
    qr = dot_nn(cq, wr_ref[...])
    per = cs_ref.shape[1]
    cos_p, sin_p = [], []
    for j in range(QB // per):
        c_t = cs_ref[j * rot:j * rot + hd, :]
        s_t = cs_ref[j * rot + hd:(j + 1) * rot, :]
        cos_p.append(jnp.concatenate([c_t] * (LANES // hd), axis=0).T)
        sin_p.append(jnp.concatenate([-s_t, s_t] * (LANES // rot), axis=0).T)
    cos_t = jnp.concatenate(cos_p, axis=0)
    sin_t = jnp.concatenate(sin_p, axis=0)
    for pr in range(GROUP // 2):
        z = qr[:, pr * LANES:(pr + 1) * LANES]
        lane = lax.broadcasted_iota(jnp.int32, z.shape, 1)
        swapped = jnp.where((lane // hd) % 2 == 0, pltpu.roll(z, LANES - hd, 1), pltpu.roll(z, hd, 1))
        zr = (z * cos_t + swapped * sin_t).astype(bf)
        for m in range(2):
            h = 2 * pr + m
            qcat[h, :, :nope] = qn[:, h * nope:(h + 1) * nope]
            qcat[h, :, nope:] = zr

    r0 = pl.multiple_of(b * QB, QB)
    tri = lax.broadcasted_iota(jnp.int32, (hb, hb), 0) <= lax.broadcasted_iota(jnp.int32, (hb, hb), 1)

    def score(h, r, slot):
        s = dot_nt(kcat[h, pl.ds(r, QB), :], qcat[h])
        sbuf[slot][...] = s
        mxb[slot][...] = jnp.max(s, axis=0, keepdims=True)

    def soft(h, slot):
        m_old = mrow[h]
        m_new = jnp.maximum(m_old, mxb[slot][...])
        alpha = jnp.exp2((m_old - m_new) * scale2)
        tot = None
        for c in range(0, QB, CH):
            p = jnp.exp2((sbuf[slot][c:c + CH, :] - m_new) * scale2)
            pbuf[slot][c:c + CH, :] = p.astype(bf)
            part = jnp.sum(p.reshape(CH // 8, 8, QB), axis=0)
            tot = part if tot is None else tot + part
        lrow[h] = lrow[h] * alpha + jnp.sum(tot, axis=0, keepdims=True)
        mrow[h] = m_new
        alb[slot][...] = alpha

    def weigh(h, r, slot):
        v = vt[h * vd:(h + 1) * vd, pl.ds(r, QB)]
        acc[h] = acc[h] * alb[slot][...] + dot_nn(v, pbuf[slot][...])

    def score_diag(h, slot):
        k = kcat[h, pl.ds(r0, QB), :]
        q = qcat[h]
        sa = dot_nt(k[:hb], q)
        sa0 = jnp.where(tri, sa[:, :hb], NEG)
        sa1 = sa[:, hb:]
        sb = jnp.where(tri, dot_nt(k[hb:], q[hb:]), NEG)
        sbuf[slot][:hb, :hb] = sa0
        sbuf[slot][:hb, hb:] = sa1
        sbuf[slot][hb:, hb:] = sb
        mxb[slot][:, :hb] = jnp.max(sa0, axis=0, keepdims=True)
        mxb[slot][:, hb:] = jnp.maximum(jnp.max(sa1, axis=0, keepdims=True), jnp.max(sb, axis=0, keepdims=True))

    def soft_diag(h, slot):
        m = mxb[slot][...]
        pa = jnp.exp2((sbuf[slot][:hb, :] - m) * scale2)
        pb = jnp.exp2((sbuf[slot][hb:, hb:] - m[:, hb:]) * scale2)
        pbuf[slot][:hb, :] = pa.astype(bf)
        pbuf[slot][hb:, hb:] = pb.astype(bf)
        la = jnp.sum(pa, axis=0, keepdims=True)
        lrow[h, :, :hb] = la[:, :hb]
        lrow[h, :, hb:] = la[:, hb:] + jnp.sum(pb, axis=0, keepdims=True)
        mrow[h] = m

    def weigh_diag(h, slot):
        rows = slice(h * vd, (h + 1) * vd)
        acc[h, :, :hb] = dot_nn(vt[rows, pl.ds(r0, hb)], pbuf[slot][:hb, :hb])
        acc[h, :, hb:] = dot_nn(vt[rows, pl.ds(r0, QB)], pbuf[slot][:, hb:])

    score_diag(0, 0)
    for h in range(GROUP):
        if h + 1 < GROUP:
            score_diag(h + 1, (h + 1) % 2)
        else:
            score(0, 0, 0)
        soft_diag(h, h % 2)
        weigh_diag(h, h % 2)

    def body(kb, _):
        r = pl.multiple_of(kb * QB, QB)
        for h in range(GROUP):
            if h + 1 < GROUP:
                score(h + 1, r, (h + 1) % 2)
            else:
                score(0, pl.multiple_of(r + QB, QB), 0)
            soft(h, h % 2)
            weigh(h, r, h % 2)
        return 0

    lax.fori_loop(0, b, body, 0)

    for h in range(GROUP):
        o_ref[:, h * vd:(h + 1) * vd] = (acc[h] * (1.0 / lrow[h])).T.astype(bf)


def attention_group(g, scale2, kv_rank, nope, rot, vd, kv_all, cq_all, cs_all, wn, wr, uk, uv):
    seq, rank = cq_all.shape
    bf = jnp.bfloat16
    f32 = jnp.float32
    pairs = seq * (seq + QB) // 2
    blocks = seq // QB
    flops = 2 * GROUP * (seq * rank * (nope + rot) + seq * kv_rank * (nope + vd) + pairs * (nope + rot + vd) * 2)
    row = pltpu.VMEM((1, QB), f32)
    return pl.pallas_call(
        functools.partial(attn_kernel, scale2, kv_rank, nope, rot),
        grid=(blocks,),
        in_specs=[
            pl.BlockSpec(kv_all.shape, lambda b: (0, 0)),
            pl.BlockSpec((QB, rank), lambda b: (b, 0)),
            pl.BlockSpec((cs_all.shape[0] // blocks, cs_all.shape[1]), lambda b: (b, 0)),
            pl.BlockSpec((rank, GROUP * nope), lambda b: (0, g)),
            pl.BlockSpec((rank, GROUP * rot), lambda b: (0, g)),
            pl.BlockSpec((kv_rank, GROUP * nope), lambda b: (0, g)),
            pl.BlockSpec((kv_rank, GROUP * vd), lambda b: (0, g)),
        ],
        out_specs=pl.BlockSpec((QB, GROUP * vd), lambda b: (b, 0)),
        out_shape=jax.ShapeDtypeStruct((seq, GROUP * vd), bf),
        scratch_shapes=[
            pltpu.VMEM((GROUP, seq, nope + LANES), bf),
            pltpu.VMEM((GROUP * vd, seq), bf),
            pltpu.VMEM((GROUP * vd, kv_rank), bf),
            pltpu.VMEM((GROUP, QB, nope + LANES), bf),
            pltpu.VMEM((GROUP, vd, QB), f32),
            pltpu.VMEM((GROUP, 1, QB), f32),
            pltpu.VMEM((GROUP, 1, QB), f32),
            pltpu.VMEM((QB, QB), f32),
            pltpu.VMEM((QB, QB), f32),
            pltpu.VMEM((QB, QB), bf),
            pltpu.VMEM((QB, QB), bf),
            row, row, row, row,
        ],
        compiler_params=pltpu.CompilerParams(dimension_semantics=("arbitrary",), vmem_limit_bytes=60_000_000),
        cost_estimate=pl.CostEstimate(flops=flops, bytes_accessed=12_000_000, transcendentals=pairs * GROUP),
        name="mla_attn",
    )(kv_all, cq_all, cs_all, wn, wr, uk, uv)


NT = 512


def out_kernel(first, *refs):
    if first:
        acc_in, (oa, ob, w_ref, out_ref) = None, refs
    else:
        acc_in, oa, ob, w_ref, out_ref = refs
    n = w_ref.shape[0]
    rows = oa.shape[0] // n
    lhs = jnp.concatenate([o[j * rows:(j + 1) * rows, :] for j in range(n) for o in (oa, ob)], axis=1)
    w = w_ref[...]
    prod = dot_nn(lhs, w.reshape(-1, w.shape[-1]))
    if not first:
        prod = prod + acc_in[...]
    out_ref[...] = prod.astype(out_ref.dtype)


def out_product(acc, oa, ob, w4, call, n):
    seq, width = oa.shape
    rows = seq // n
    hidden = w4.shape[3]
    first = acc is None
    tile = pl.BlockSpec((rows, NT), lambda s: (0, s))
    full = pl.BlockSpec((seq, width), lambda s: (0, 0))
    args = ([] if first else [acc]) + [oa, ob, w4]
    return pl.pallas_call(
        functools.partial(out_kernel, first),
        grid=(hidden // NT,),
        in_specs=([] if first else [tile]) + [full, full, pl.BlockSpec((n, 2, width, NT), lambda s: (0, call, 0, s))],
        out_specs=tile,
        out_shape=jax.ShapeDtypeStruct((rows, hidden), jnp.float32 if first else jnp.bfloat16),
        compiler_params=pltpu.CompilerParams(dimension_semantics=("arbitrary",), vmem_limit_bytes=60_000_000),
        cost_estimate=pl.CostEstimate(flops=4 * rows * hidden * width * n, bytes_accessed=4 * hidden * width * n, transcendentals=0),
        name="out_product",
    )(*args)


def solution(mesh):
    n = mesh.shape['sp']
    rows_spec = P(('dp', 'sp'), None)
    tok_spec = P(('dp', 'sp'))
    rep = P()

    def local_step(tok_in, tok_pos, w_dq, g_q, w_uq, w_dkv, g_kv, w_uk, w_uv, w_o):
        num_heads = w_uq.shape[1]
        heads = num_heads // n
        qk_dim = w_uq.shape[2]
        kv_rank = g_kv.shape[0]
        rot = w_dkv.shape[1] - kv_rank
        nope = qk_dim - rot
        vd = w_uv.shape[2]
        scale2 = (0.1 * math.log(YARN_FACTOR) + 1.0) ** 2 / math.sqrt(qk_dim) / math.log(2.0)

        angles = tok_pos.astype(jnp.float32)[:, None] * rope_freqs(rot)[None, :]
        cos_t, sin_t = jnp.cos(angles), jnp.sin(angles)
        cs_own = jnp.concatenate([cos_t, sin_t], axis=1).T
        cq_own, cache_kv, cache_pe, kv_own = latents(tok_in, w_dq, w_dkv, g_q, g_kv, cos_t, sin_t)

        w_t = jnp.transpose(w_uq, (0, 2, 1))
        kv_all, cs_all, cq_all, wn, wr, uk, uv = gather_and_pick(n, heads, nope, kv_own, cs_own, cq_own, w_t, w_uk, w_uv)

        chunks = heads // GROUP
        o_parts = []
        for g in range(chunks):
            o_g = attention_group(g, scale2, kv_rank, nope, rot, vd, kv_all, cq_all, cs_all, wn, wr, uk, uv)
            o_parts.append(lax.all_to_all(o_g, 'sp', 0, 0, tiled=True))
        w4 = w_o.reshape(n, chunks, GROUP * vd, w_o.shape[2])
        acc = None
        for call in range(chunks // 2):
            acc = out_product(acc, o_parts[2 * call], o_parts[2 * call + 1], w4, call, n)
        return acc, cache_kv, cache_pe

    return jax.shard_map(local_step, mesh=mesh, in_specs=(rows_spec, tok_spec, rep, rep, rep, rep, rep, rep, rep, rep), out_specs=(rows_spec, rows_spec, rows_spec), check_vma=False)
```

time: 954 us -> 322 us (0.34); the launches traced: 939 us -> 320 us
  matrix products: 467 us -> 0 us
  waiting for transfers between devices: 308 us -> 0.01 us
  Pallas kernels: 0 us -> 296 us
  local copies, waits for them, and re-layouts: 106 us -> 3.51 us
  other arithmetic: 26.9 us -> 2.16 us
    all_to_all x4, waiting for transfers between devices: 308 us -> 0.01 us  [local_step(): o_parts.append(lax.all_to_all(o_g, 'sp', 0, 0, tiled=True))]
    dot_general x13 -> x0, matrix products: 299 us -> none  [the longest x8 124 us: block_attention(): jnp.einsum('hqk,khv->qhv', attn_prob, v_heads, preferred_element_type=jnp...]
    pallas_call x0 -> x8, Pallas kernels: none -> 296 us  [the longest x4 128 us: attention_group(): pl.pallas_call(functools.partial(attn_kernel, scale2, kv_rank, nope, rot)...]
    sub x8 -> x0, matrix products: 159 us -> none  [block_attention(): attn_prob = jax.nn.softmax(logits, axis=-1).astype(jnp.bfloat16)]
    all_to_all x4 -> x0, local copies, waits for them, and re-layouts: 38.3 us -> none  [the longest x1 10.8 us: local_step(): q_heads = lax.all_to_all(q_all, 'sp', 1, 0, tiled=True)]
    unnamed x16 -> x7, local copies, waits for them, and re-layouts: 25.8 us -> 0.72 us
    concatenate x3 -> x0, other arithmetic: 17.2 us -> none  [the longest x1 8.81 us: local_step(): jnp.concatenate([k_nope, jnp.broadcast_to(cache_pe[:, None, :], (rows, nu...]
    concatenate x1 -> x0, local copies, waits for them, and re-layouts: 17 us -> none  [local_step(): jnp.concatenate([q_full[:, :, :nope_dim], rotate_half(q_full[:, :, nope_d...]
  transfers between devices with their start and end apart: 4 -> 4, of which waited for: 3 -> 0; matrix products, arithmetic and copies ran while one was open for 18% -> 0% of each run, Pallas kernels for 0% -> 45%
where the time goes in v2:
time: 322 us; the launch traced here: 320 us
  Pallas kernels  296 us (92%)
  starting transfers between devices  18.3 us (6%)
  local copies, waits for them, and re-layouts  3.51 us (1%)
    pallas_call x4, Pallas kernels, attention_group(): pl.pallas_call(functools.partial(attn_kernel, scale2, kv_rank, nope, rot)...  128 us
    pallas_call x2, Pallas kernels, out_product(): pl.pallas_call(functools.partial(out_kernel, first), grid=(hidden // NT,)...  95.3 us
    pallas_call x1, Pallas kernels, gather_and_pick(): pl.pallas_call(functools.partial(gather_kernel, n, heads, nope), grid=(st...  51.2 us
    pallas_call x1, Pallas kernels, latents(): pl.pallas_call(functools.partial(latent_kernel, kv_rank), grid=(hidden //...  21 us
    all_to_all x4, starting transfers between devices, local_step(): o_parts.append(lax.all_to_all(o_g, 'sp', 0, 0, tiled=True))  18.3 us
  transfers between devices with their start and end apart: 4, of which 0 were waited for; matrix products, arithmetic and copies ran while one was open for 0% of the time, Pallas kernels for 45%

profile of v2, /device:TPU:81, one launch (start us, length us, event | category | flops | bytes accessed | tf_op | source)
XLA Modules:
  0.0 320.3 jit_solution(5768788360690983774)
XLA Ops:
  0.6 0.7 convert_element_type.3
  1.3 0.8 multiply_sine_fusion
  2.2 0.8 copy.14.cos_ref
  2.9 0.6 maximum_bitcast_fusion.cs_ref
  3.5 0.7 copy.15.sin_ref
  4.3 1.3 broadcast_in_dim.8.gq_ref
  5.6 21.0 %latents.1 = (bf16[256,1536]{1,0:T(8,128)(2,1)}, bf16[256,512]{1,0:T(8,128)(2,1)}, bf16[256,64]{1,0:T(8,128)(2,1)}, bf16[256,640]{1,0:T(8,128)(2,1)}) custom-call(bf16[256,7168]{1,0:T(8,128)(2,1)} %x_ref.1, bf16[7168,1536]{1,0:T(8,128)(2,1)} %wq_ref.1, bf16[576,7168]{1,0:T(8,128)(2,1)} %bitcast.16, f32[1,1536]{1,0:T(1,128)} %broadcast_in_dim.8.gq_ref, ...), custom_call_target="tpu_custom_call" | custom-call | flops 7751073792 | bytes 33947648 | tf_op jit(solution)/shard_map/latents/pallas_call | solution.py:89
  26.5 51.2 %gather_pick.1 = (bf16[2048,640]{1,0:T(8,128)(2,1)}, f32[512,256]{1,0:T(8,128)}, bf16[2048,1536]{1,0:T(8,128)(2,1)}, bf16[1536,2048]{1,0:T(8,128)(2,1)}, bf16[15...) custom-call(bf16[256,640]{1,0:T(8,128)(2,1)} %get-tuple-element.14.kv_ref, ...), custom_call_target="tpu_custom_call" | custom-call | flops 30000001024 | bytes 90000000 | tf_op jit(solution)/shard_map/gather_pick/pallas_call | solution.py:258
  77.7 32.1 %mla_attn.7 = bf16[2048,512]{1,0:T(8,128)(2,1)} custom-call(bf16[2048,640]{1,0:T(8,128)(2,1)} %get-tuple-element.16.kv_ref, bf16[2048,1536]{1,0:T(8,128)(2,1)} %get-tuple-element.17.cq_ref, f32[512,256]{1,0:T(8,128)} %get-tuple-element.18.cs_ref, bf16[1536,2048]{1,0:T(8,128)(2,1)} %get-tuple-element.19.wn_ref, bf16[1536,1024]{1,0:T(8,128)(2,1)} %get-tuple-element.20.wr_ref, ...), custom_call_target="tpu_custom_call" | custom-call | flops 20401094656 | bytes 12000000 | tf_op jit(solution)/shard_map/mla_attn/pallas_call | solution.py:442
  109.8 4.0 %all-to-all-start.3 = ((bf16[8,256,512]{2,1,0:T(8,128)(2,1)}), bf16[8,256,512]{2,1,0:T(8,128)(2,1)S(1)}, u32[]{:S(2)}, u32[]{:S(2)}) async-start(bf16[8,256,512]{2,1,0:T(8,128)(2,1)} %bitcast.20), calls=%async_computation.3 | async-start | bytes 4194304 | tf_op jit(solution)/shard_map/all_to_all | solution.py:542
  113.8 0.7 copy.16
  114.5 32.1 %mla_attn.5 = bf16[2048,512]{1,0:T(8,128)(2,1)} custom-call(bf16[2048,640]{1,0:T(8,128)(2,1)} %get-tuple-element.16.kv_ref, bf16[2048,1536]{1,0:T(8,128)(2,1)} %get-tuple-element.17.cq_ref, f32[512,256]{1,0:T(8,128)} %get-tuple-element.18.cs_ref, bf16[1536,2048]{1,0:T(8,128)(2,1)} %get-tuple-element.19.wn_ref, bf16[1536,1024]{1,0:T(8,128)(2,1)} %get-tuple-element.20.wr_ref, ...), custom_call_target="tpu_custom_call" | custom-call | flops 20401094656 | bytes 12000000 | tf_op jit(solution)/shard_map/mla_attn/pallas_call | solution.py:442
  146.6 0.0 all-to-all-done.3
  146.6 4.7 %all-to-all-start.1 = ((bf16[8,256,512]{2,1,0:T(8,128)(2,1)}), bf16[8,256,512]{2,1,0:T(8,128)(2,1)}, u32[]{:S(2)}, u32[]{:S(2)}) async-start(bf16[8,256,512]{2,1,0:T(8,128)(2,1)} %bitcast.19), calls=%async_computation.1 | async-start | bytes 4194304 | tf_op jit(solution)/shard_map/all_to_all | solution.py:542
  151.3 32.1 %mla_attn.4 = bf16[2048,512]{1,0:T(8,128)(2,1)} custom-call(bf16[2048,640]{1,0:T(8,128)(2,1)} %get-tuple-element.16.kv_ref, bf16[2048,1536]{1,0:T(8,128)(2,1)} %get-tuple-element.17.cq_ref, f32[512,256]{1,0:T(8,128)} %get-tuple-element.18.cs_ref, bf16[1536,2048]{1,0:T(8,128)(2,1)} %get-tuple-element.19.wn_ref, bf16[1536,1024]{1,0:T(8,128)(2,1)} %get-tuple-element.20.wr_ref, ...), custom_call_target="tpu_custom_call" | custom-call | flops 20401094656 | bytes 12000000 | tf_op jit(solution)/shard_map/mla_attn/pallas_call | solution.py:442
  183.3 0.0 copy-done
  183.3 0.0 all-to-all-done.1
  183.3 4.8 %all-to-all-start = ((bf16[8,256,512]{2,1,0:T(8,128)(2,1)}), bf16[8,256,512]{2,1,0:T(8,128)(2,1)S(1)}, u32[]{:S(2)}, u32[]{:S(2)}) async-start(bf16[8,256,512]{2,1,0:T(8,128)(2,1)} %bitcast.18), calls=%async_computation | async-start | bytes 4194304 | tf_op jit(solution)/shard_map/all_to_all | solution.py:542
  188.2 32.1 %mla_attn.6 = bf16[2048,512]{1,0:T(8,128)(2,1)} custom-call(bf16[2048,640]{1,0:T(8,128)(2,1)} %get-tuple-element.16.kv_ref, bf16[2048,1536]{1,0:T(8,128)(2,1)} %get-tuple-element.17.cq_ref, f32[512,256]{1,0:T(8,128)} %get-tuple-element.18.cs_ref, bf16[1536,2048]{1,0:T(8,128)(2,1)} %get-tuple-element.19.wn_ref, bf16[1536,1024]{1,0:T(8,128)(2,1)} %get-tuple-element.20.wr_ref, ...), custom_call_target="tpu_custom_call" | custom-call | flops 20401094656 | bytes 12000000 | tf_op jit(solution)/shard_map/mla_attn/pallas_call | solution.py:442
  220.2 0.0 all-to-all-done
  220.2 4.8 %all-to-all-start.2 = ((bf16[8,256,512]{2,1,0:T(8,128)(2,1)}), bf16[8,256,512]{2,1,0:T(8,128)(2,1)}, u32[]{:S(2)}, u32[]{:S(2)}) async-start(bf16[8,256,512]{2,1,0:T(8,128)(2,1)} %bitcast.17), calls=%async_computation.2 | async-start | bytes 4194304 | tf_op jit(solution)/shard_map/all_to_all | solution.py:542
  225.1 47.3 %out_product.2.refs_0_ = f32[256,7168]{1,0:T(8,128)} custom-call(bf16[2048,512]{1,0:T(8,128)(2,1)} %bitcast.15, bf16[2048,512]{1,0:T(8,128)(2,1)} %bitcast.7.refs_1_, bf16[8,4,512,7168]{3,2,1,0:T(8,128)(2,1)} %bitcast.8.refs_2_.refs_3_), custom_call_target="tpu_custom_call" | custom-call | flops 30064771072 | bytes 117440512 | tf_op jit(solution)/shard_map/out_product/pallas_call | solution.py:502
  272.4 0.0 all-to-all-done.2
  272.4 48.0 %out_product.3 = bf16[256,7168]{1,0:T(8,128)(2,1)} custom-call(f32[256,7168]{1,0:T(8,128)} %out_product.2.refs_0_, bf16[2048,512]{1,0:T(8,128)(2,1)} %bitcast.10.refs_1_, bf16[2048,512]{1,0:T(8,128)(2,1)} %bitcast.14, bf16[8,4,512,7168]{3,2,1,0:T(8,128)(2,1)} %bitcast.8.refs_2_.refs_3_), custom_call_target="tpu_custom_call" | custom-call | flops 30064771072 | bytes 117440512 | tf_op jit(solution)/shard_map/out_product/pallas_call | solution.py:502
  (5 shorter events, 0.0 us)
Async XLA Ops:
  109.8 4.0 %copy-start.2 = (bf16[256,64]{1,0:T(8,128)(2,1)S(1)}, bf16[256,64]{1,0:T(8,128)(2,1)}, u32[]{:S(2)}) copy-start(bf16[256,64]{1,0:T(8,128)(2,1)} %get-tuple-element.27) | copy-start | bytes 98308
  109.8 36.8 %all-to-all-start.3 = ((bf16[8,256,512]{2,1,0:T(8,128)(2,1)}), bf16[8,256,512]{2,1,0:T(8,128)(2,1)S(1)}, u32[]{:S(2)}, u32[]{:S(2)}) async-start(bf16[8,256,512]{2,1,0:T(8,128)(2,1)} %bitcast.20), calls=%async_computation.3 | async-start | bytes 4194304 | tf_op jit(solution)/shard_map/all_to_all | solution.py:542
  146.6 36.8 %copy-start = (bf16[8,256,512]{2,1,0:T(8,128)(2,1)}, bf16[8,256,512]{2,1,0:T(8,128)(2,1)S(1)}, u32[]{:S(2)}) copy-start(bf16[8,256,512]{2,1,0:T(8,128)(2,1)S(1)} %all-to-all-done.3) | copy-start | bytes 6291460
  146.6 36.7 %all-to-all-start.1 = ((bf16[8,256,512]{2,1,0:T(8,128)(2,1)}), bf16[8,256,512]{2,1,0:T(8,128)(2,1)}, u32[]{:S(2)}, u32[]{:S(2)}) async-start(bf16[8,256,512]{2,1,0:T(8,128)(2,1)} %bitcast.19), calls=%async_computation.1 | async-start | bytes 4194304 | tf_op jit(solution)/shard_map/all_to_all | solution.py:542
  183.3 36.9 %all-to-all-start = ((bf16[8,256,512]{2,1,0:T(8,128)(2,1)}), bf16[8,256,512]{2,1,0:T(8,128)(2,1)S(1)}, u32[]{:S(2)}, u32[]{:S(2)}) async-start(bf16[8,256,512]{2,1,0:T(8,128)(2,1)} %bitcast.18), calls=%async_computation | async-start | bytes 4194304 | tf_op jit(solution)/shard_map/all_to_all | solution.py:542
  220.2 4.8 %copy-start.1 = (bf16[8,256,512]{2,1,0:T(8,128)(2,1)}, bf16[8,256,512]{2,1,0:T(8,128)(2,1)S(1)}, u32[]{:S(2)}) copy-start(bf16[8,256,512]{2,1,0:T(8,128)(2,1)S(1)} %all-to-all-done) | copy-start | bytes 6291460
  220.2 52.1 %all-to-all-start.2 = ((bf16[8,256,512]{2,1,0:T(8,128)(2,1)}), bf16[8,256,512]{2,1,0:T(8,128)(2,1)}, u32[]{:S(2)}, u32[]{:S(2)}) async-start(bf16[8,256,512]{2,1,0:T(8,128)(2,1)} %bitcast.17), calls=%async_computation.2 | async-start | bytes 4194304 | tf_op jit(solution)/shard_map/all_to_all | solution.py:542

commit v3 on v2

--- a/solution.py
+++ b/solution.py
@@ -53,27 +53,50 @@
     return jnp.dot(a, b, preferred_element_type=jnp.float32)
 
 
-def latent_kernel(kv_rank, x_ref, wq_ref, wkvt_ref, gq_ref, gkv_ref, cos_ref, sin_ref, cq_ref, kv_ref, pe_ref, own_ref, acc_q, acc_kv):
-    step = pl.program_id(0)
+LK = 512
+LSLOTS = 6
+
+
+def latent_kernel(kv_rank, x_ref, wq_ref, wkvt_ref, gq_ref, gkv_ref, cos_ref, sin_ref, cq_ref, kv_ref, pe_ref, own_ref, xb, qb, kb, acc_q, acc_kv, sem):
     bf = jnp.bfloat16
-
-    @pl.when(step == 0)
-    def _():
-        acc_q[...] = jnp.zeros_like(acc_q)
-        acc_kv[...] = jnp.zeros_like(acc_kv)
-
-    acc_q[...] += dot_nn(x_ref[...], wq_ref[...])
-    acc_kv[...] += dot_nt(x_ref[...], wkvt_ref[...])
-
-    @pl.when(step == pl.num_programs(0) - 1)
-    def _():
-        cq_ref[...] = rms_norm(acc_q[...], gq_ref[...]).astype(bf)
-        lat = rms_norm(acc_kv[:, :kv_rank], gkv_ref[...]).astype(bf)
-        kv_ref[...] = lat
-        pe = rotate_half(acc_kv[:, kv_rank:], cos_ref[...], sin_ref[...]).astype(bf)
-        pe_ref[...] = pe
-        own_ref[:, :kv_rank] = lat
-        own_ref[:, kv_rank:] = jnp.concatenate([pe, jnp.zeros((pe.shape[0], LANES - pe.shape[1]), bf)], axis=1)
+    steps = x_ref.shape[1] // LK
+
+    def copies(s, slot):
+        k = pl.ds(pl.multiple_of(s * LK, LK), LK)
+        return (
+            pltpu.make_async_copy(x_ref.at[:, k], xb.at[slot], sem.at[0, slot]),
+            pltpu.make_async_copy(wq_ref.at[k, :], qb.at[slot], sem.at[1, slot]),
+            pltpu.make_async_copy(wkvt_ref.at[:, k], kb.at[slot], sem.at[2, slot]),
+        )
+
+    for s in range(LSLOTS - 1):
+        for c in copies(s, s):
+            c.start()
+    acc_q[...] = jnp.zeros_like(acc_q)
+    acc_kv[...] = jnp.zeros_like(acc_kv)
+
+    def body(s, _):
+        slot = lax.rem(s, LSLOTS)
+
+        @pl.when(s + LSLOTS - 1 < steps)
+        def _():
+            for c in copies(s + LSLOTS - 1, lax.rem(s + LSLOTS - 1, LSLOTS)):
+                c.start()
+        for c in copies(s, slot):
+            c.wait()
+        x = xb[slot]
+        acc_q[...] += dot_nn(x, qb[slot])
+        acc_kv[...] += dot_nt(x, kb[slot])
+        return 0
+
+    lax.fori_loop(0, steps, body, 0)
+    cq_ref[...] = rms_norm(acc_q[...], gq_ref[...]).astype(bf)
+    lat = rms_norm(acc_kv[:, :kv_rank], gkv_ref[...]).astype(bf)
+    kv_ref[...] = lat
+    pe = rotate_half(acc_kv[:, kv_rank:], cos_ref[...], sin_ref[...]).astype(bf)
+    pe_ref[...] = pe
+    own_ref[:, :kv_rank] = lat
+    own_ref[:, kv_rank:] = jnp.concatenate([pe, jnp.zeros((pe.shape[0], LANES - pe.shape[1]), bf)], axis=1)
 
 
 def latents(x, w_dq, w_dkv, g_q, g_kv, cos_t, sin_t):
@@ -82,43 +105,35 @@
     kvw = w_dkv.shape[1]
     kv_rank = g_kv.shape[0]
     rot = kvw - kv_rank
-    half = rot // 2
-    kb = 512
     bf = jnp.bfloat16
-    const = lambda s: (0, 0)
+    anyspec = pl.BlockSpec(memory_space=pl.ANY)
+    vm = pl.BlockSpec(memory_space=pltpu.VMEM)
     return pl.pallas_call(
         functools.partial(latent_kernel, kv_rank),
-        grid=(hidden // kb,),
-        in_specs=[
-            pl.BlockSpec((rows, kb), lambda s: (0, s)),
-            pl.BlockSpec((kb, rank), lambda s: (s, 0)),
-            pl.BlockSpec((kvw, kb), lambda s: (0, s)),
-            pl.BlockSpec((1, rank), const),
-            pl.BlockSpec((1, kv_rank), const),
-            pl.BlockSpec((rows, half), const),
-            pl.BlockSpec((rows, half), const),
-        ],
-        out_specs=[
-            pl.BlockSpec((rows, rank), const),
-            pl.BlockSpec((rows, kv_rank), const),
-            pl.BlockSpec((rows, rot), const),
-            pl.BlockSpec((rows, kv_rank + LANES), const),
-        ],
+        in_specs=[anyspec] * 3 + [vm] * 4,
+        out_specs=[vm] * 4,
         out_shape=[
             jax.ShapeDtypeStruct((rows, rank), bf),
             jax.ShapeDtypeStruct((rows, kv_rank), bf),
             jax.ShapeDtypeStruct((rows, rot), bf),
             jax.ShapeDtypeStruct((rows, kv_rank + LANES), bf),
         ],
-        scratch_shapes=[pltpu.VMEM((rows, rank), jnp.float32), pltpu.VMEM((rows, kvw), jnp.float32)],
-        compiler_params=pltpu.CompilerParams(dimension_semantics=("arbitrary",)),
+        scratch_shapes=[
+            pltpu.VMEM((LSLOTS, rows, LK), bf),
+            pltpu.VMEM((LSLOTS, LK, rank), bf),
+            pltpu.VMEM((LSLOTS, kvw, LK), bf),
+            pltpu.VMEM((rows, rank), jnp.float32),
+            pltpu.VMEM((rows, kvw), jnp.float32),
+            pltpu.SemaphoreType.DMA((3, LSLOTS)),
+        ],
+        compiler_params=pltpu.CompilerParams(vmem_limit_bytes=60_000_000),
         cost_estimate=pl.CostEstimate(flops=2 * rows * hidden * (rank + kvw), bytes_accessed=2 * hidden * (rank + kvw + rows), transcendentals=0),
         name="latents",
     )(x, w_dq, w_dkv.T, g_q[None, :], g_kv[None, :], cos_t, sin_t)
 
 
 SUB = 16
-CBLK = 96
+CBLK = 192
 
 
 def gather_kernel(n, heads, nope, kv_ref, cs_ref, cq_ref, wt_ref, uk_ref, uv_ref, kv_all, cs_all, cq_all, wn_ref, wr_ref, uko_ref, uvo_ref, sel, tn, tr, tu, send_sem, recv_sem, loc_sem):
@@ -190,12 +205,29 @@
         for c in range(SUB):
             sel[c * lanes:(c + 1) * lanes, :] = jnp.where(code == c, 1.0, 0.0).astype(bf)
 
-    @pl.when(step == last // 2)
+    def hand_on(arr):
+        cps[arr][0].wait_recv()
+        cps[arr][5].start()
+        cps[arr][2].wait_recv()
+        cps[arr][6].start()
+
+    def to_mate(arr):
+        cps[arr][1].wait_recv()
+        cps[arr][7].start()
+        cps[arr][3].wait_recv()
+        cps[arr][8].start()
+
+    @pl.when(step == (3 * last) // 7)
     def _():
-        cps[2][0].wait_recv()
-        cps[2][5].start()
-        cps[2][2].wait_recv()
-        cps[2][6].start()
+        hand_on(2)
+
+    @pl.when(step == (5 * last) // 7)
+    def _():
+        to_mate(2)
+
+    @pl.when(step == last)
+    def _():
+        hand_on(0)
 
     for s in range(CBLK // SUB):
         lhs = jnp.concatenate([wt_ref[s * SUB + i] for i in range(SUB)], axis=1)
@@ -217,20 +249,9 @@
 
     @pl.when(step == last)
     def _():
-        cps[2][1].wait_recv()
-        cps[2][7].start()
-        cps[2][3].wait_recv()
-        cps[2][8].start()
-        for arr in (0, 1):
-            cps[arr][0].wait_recv()
-            cps[arr][5].start()
-            cps[arr][2].wait_recv()
-            cps[arr][6].start()
-        for arr in (0, 1):
-            cps[arr][1].wait_recv()
-            cps[arr][7].start()
-            cps[arr][3].wait_recv()
-            cps[arr][8].start()
+        hand_on(1)
+        to_mate(0)
+        to_mate(1)
         for arr in (2, 0, 1):
             cps[arr][5].wait_recv()
             cps[arr][9].start()
@@ -473,22 +494,50 @@
     )(kv_all, cq_all, cs_all, wn, wr, uk, uv)
 
 
-NT = 512
-
-
-def out_kernel(first, *refs):
+OSLOTS = 3
+NT = 1024
+
+
+def out_kernel(n, call, first, *refs):
     if first:
-        acc_in, (oa, ob, w_ref, out_ref) = None, refs
+        oa, ob, w_ref, out_ref, wbuf, acc, sem, acc_sem = refs
     else:
-        acc_in, oa, ob, w_ref, out_ref = refs
-    n = w_ref.shape[0]
+        acc_in, oa, ob, w_ref, out_ref, wbuf, acc, sem, acc_sem = refs
     rows = oa.shape[0] // n
-    lhs = jnp.concatenate([o[j * rows:(j + 1) * rows, :] for j in range(n) for o in (oa, ob)], axis=1)
-    w = w_ref[...]
-    prod = dot_nn(lhs, w.reshape(-1, w.shape[-1]))
-    if not first:
-        prod = prod + acc_in[...]
-    out_ref[...] = prod.astype(out_ref.dtype)
+    hidden = w_ref.shape[3]
+    steps = 2 * n
+
+    def copy(s, slot):
+        return pltpu.make_async_copy(w_ref.at[lax.rem(s, n), 2 * call + s // n], wbuf.at[slot], sem.at[slot])
+
+    for s in range(OSLOTS - 1):
+        copy(s, s).start()
+    if first:
+        acc[...] = jnp.zeros_like(acc)
+    else:
+        pltpu.make_async_copy(acc_in, acc, acc_sem).start()
+        pltpu.make_async_copy(acc_in, acc, acc_sem).wait()
+
+    def body(s, _):
+        slot = lax.rem(s, OSLOTS)
+
+        @pl.when(s + OSLOTS - 1 < steps)
+        def _():
+            copy(s + OSLOTS - 1, lax.rem(s + OSLOTS - 1, OSLOTS)).start()
+        copy(s, slot).wait()
+        r = pl.ds(pl.multiple_of(lax.rem(s, n) * rows, rows), rows)
+        lhs = jnp.where(s < n, oa[r, :], ob[r, :])
+        for t in range(hidden // NT):
+            cols = slice(t * NT, (t + 1) * NT)
+            acc[:, cols] += dot_nn(lhs, wbuf[slot, :, cols])
+        return 0
+
+    lax.fori_loop(0, steps, body, 0)
+    if first:
+        pltpu.make_async_copy(acc, out_ref, acc_sem).start()
+        pltpu.make_async_copy(acc, out_ref, acc_sem).wait()
+    else:
+        out_ref[...] = acc[...].astype(out_ref.dtype)
 
 
 def out_product(acc, oa, ob, w4, call, n):
@@ -496,16 +545,21 @@
     rows = seq // n
     hidden = w4.shape[3]
     first = acc is None
-    tile = pl.BlockSpec((rows, NT), lambda s: (0, s))
-    full = pl.BlockSpec((seq, width), lambda s: (0, 0))
+    anyspec = pl.BlockSpec(memory_space=pl.ANY)
+    vm = pl.BlockSpec(memory_space=pltpu.VMEM)
     args = ([] if first else [acc]) + [oa, ob, w4]
     return pl.pallas_call(
-        functools.partial(out_kernel, first),
-        grid=(hidden // NT,),
-        in_specs=([] if first else [tile]) + [full, full, pl.BlockSpec((n, 2, width, NT), lambda s: (0, call, 0, s))],
-        out_specs=tile,
+        functools.partial(out_kernel, n, call, first),
+        in_specs=([] if first else [anyspec]) + [vm, vm, anyspec],
+        out_specs=anyspec if first else vm,
         out_shape=jax.ShapeDtypeStruct((rows, hidden), jnp.float32 if first else jnp.bfloat16),
-        compiler_params=pltpu.CompilerParams(dimension_semantics=("arbitrary",), vmem_limit_bytes=60_000_000),
+        scratch_shapes=[
+            pltpu.VMEM((OSLOTS, width, hidden), jnp.bfloat16),
+            pltpu.VMEM((rows, hidden), jnp.float32),
+            pltpu.SemaphoreType.DMA((OSLOTS,)),
+            pltpu.SemaphoreType.DMA,
+        ],
+        compiler_params=pltpu.CompilerParams(vmem_limit_bytes=60_000_000),
         cost_estimate=pl.CostEstimate(flops=4 * rows * hidden * width * n, bytes_accessed=4 * hidden * width * n, transcendentals=0),
         name="out_product",
     )(*args)

time: 322 us -> 307 us (0.953)
  Pallas kernels: 296 us -> 282 us
    pallas_call x3, Pallas kernels: 116 us -> 103 us  [the longest x2 87.7 us: out_product(): pl.pallas_call(functools.partial(out_kernel, n, call, first), in_specs=([...]
where the time goes in v3:
time: 307 us
  Pallas kernels  282 us (92%)
  starting transfers between devices  18.3 us (6%)
  local copies, waits for them, and re-layouts  3.51 us (1%)
    pallas_call x4, Pallas kernels, attention_group(): pl.pallas_call(functools.partial(attn_kernel, scale2, kv_rank, nope, rot)...  128 us
    pallas_call x2, Pallas kernels, out_product(): pl.pallas_call(functools.partial(out_kernel, n, call, first), in_specs=([...  87.7 us
    pallas_call x1, Pallas kernels, gather_and_pick(): pl.pallas_call(functools.partial(gather_kernel, n, heads, nope), grid=(st...  50.7 us
    all_to_all x4, starting transfers between devices, local_step(): o_parts.append(lax.all_to_all(o_g, 'sp', 0, 0, tiled=True))  18.3 us
    pallas_call x1, Pallas kernels, latents(): pl.pallas_call(functools.partial(latent_kernel, kv_rank), in_specs=[anysp...  15.2 us
  transfers between devices with their start and end apart: 4, of which 0 were waited for; matrix products, arithmetic and copies ran while one was open for 0% of the time, Pallas kernels for 45%

profile of v3, /device:TPU:81, one launch (start us, length us, event | category | flops | bytes accessed | tf_op | source)
XLA Modules:
  0.0 306.8 jit_solution(16850412120643946463)
XLA Ops:
  0.6 0.7 convert_element_type.3
  1.3 0.8 multiply_sine_fusion
  2.2 0.8 copy.14.cos_ref
  2.9 0.6 maximum_bitcast_fusion.cs_ref
  3.5 0.7 copy.15.sin_ref
  4.3 1.3 broadcast_in_dim.8.gq_ref
  5.6 15.2 %latents.1 = (bf16[256,1536]{1,0:T(8,128)(2,1)}, bf16[256,512]{1,0:T(8,128)(2,1)}, bf16[256,64]{1,0:T(8,128)(2,1)}, bf16[256,640]{1,0:T(8,128)(2,1)}) custom-call(bf16[256,7168]{1,0:T(8,128)(2,1)} %x_ref.1, bf16[7168,1536]{1,0:T(8,128)(2,1)} %wq_ref.1, bf16[576,7168]{1,0:T(8,128)(2,1)} %bitcast.16, f32[1,1536]{1,0:T(1,128)} %broadcast_in_dim.8.gq_ref, ...), custom_call_target="tpu_custom_call" | custom-call | flops 7751073792 | bytes 33947648 | tf_op jit(solution)/shard_map/latents/pallas_call | solution.py:111
  20.8 50.7 %gather_pick.1 = (bf16[2048,640]{1,0:T(8,128)(2,1)}, f32[512,256]{1,0:T(8,128)}, bf16[2048,1536]{1,0:T(8,128)(2,1)}, bf16[1536,2048]{1,0:T(8,128)(2,1)}, bf16[15...) custom-call(bf16[256,640]{1,0:T(8,128)(2,1)} %get-tuple-element.14.kv_ref, ...), custom_call_target="tpu_custom_call" | custom-call | flops 30000001024 | bytes 90000000 | tf_op jit(solution)/shard_map/gather_pick/pallas_call | solution.py:279
  71.6 32.1 %mla_attn.7 = bf16[2048,512]{1,0:T(8,128)(2,1)} custom-call(bf16[2048,640]{1,0:T(8,128)(2,1)} %get-tuple-element.16.kv_ref, bf16[2048,1536]{1,0:T(8,128)(2,1)} %get-tuple-element.17.cq_ref, f32[512,256]{1,0:T(8,128)} %get-tuple-element.18.cs_ref, bf16[1536,2048]{1,0:T(8,128)(2,1)} %get-tuple-element.19.wn_ref, bf16[1536,1024]{1,0:T(8,128)(2,1)} %get-tuple-element.20.wr_ref, ...), custom_call_target="tpu_custom_call" | custom-call | flops 20401094656 | bytes 12000000 | tf_op jit(solution)/shard_map/mla_attn/pallas_call | solution.py:463
  103.6 4.0 %all-to-all-start.3 = ((bf16[8,256,512]{2,1,0:T(8,128)(2,1)}), bf16[8,256,512]{2,1,0:T(8,128)(2,1)S(1)}, u32[]{:S(2)}, u32[]{:S(2)}) async-start(bf16[8,256,512]{2,1,0:T(8,128)(2,1)} %bitcast.20), calls=%async_computation.3 | async-start | bytes 4194304 | tf_op jit(solution)/shard_map/all_to_all | solution.py:596
  107.7 0.0 copy-done.2
  107.7 0.7 copy.16
  108.4 32.1 %mla_attn.5 = bf16[2048,512]{1,0:T(8,128)(2,1)} custom-call(bf16[2048,640]{1,0:T(8,128)(2,1)} %get-tuple-element.16.kv_ref, bf16[2048,1536]{1,0:T(8,128)(2,1)} %get-tuple-element.17.cq_ref, f32[512,256]{1,0:T(8,128)} %get-tuple-element.18.cs_ref, bf16[1536,2048]{1,0:T(8,128)(2,1)} %get-tuple-element.19.wn_ref, bf16[1536,1024]{1,0:T(8,128)(2,1)} %get-tuple-element.20.wr_ref, ...), custom_call_target="tpu_custom_call" | custom-call | flops 20401094656 | bytes 12000000 | tf_op jit(solution)/shard_map/mla_attn/pallas_call | solution.py:463
  140.4 0.0 all-to-all-done.3
  140.4 4.7 %all-to-all-start.1 = ((bf16[8,256,512]{2,1,0:T(8,128)(2,1)}), bf16[8,256,512]{2,1,0:T(8,128)(2,1)}, u32[]{:S(2)}, u32[]{:S(2)}) async-start(bf16[8,256,512]{2,1,0:T(8,128)(2,1)} %bitcast.19), calls=%async_computation.1 | async-start | bytes 4194304 | tf_op jit(solution)/shard_map/all_to_all | solution.py:596
  145.1 32.1 %mla_attn.4 = bf16[2048,512]{1,0:T(8,128)(2,1)} custom-call(bf16[2048,640]{1,0:T(8,128)(2,1)} %get-tuple-element.16.kv_ref, bf16[2048,1536]{1,0:T(8,128)(2,1)} %get-tuple-element.17.cq_ref, f32[512,256]{1,0:T(8,128)} %get-tuple-element.18.cs_ref, bf16[1536,2048]{1,0:T(8,128)(2,1)} %get-tuple-element.19.wn_ref, bf16[1536,1024]{1,0:T(8,128)(2,1)} %get-tuple-element.20.wr_ref, ...), custom_call_target="tpu_custom_call" | custom-call | flops 20401094656 | bytes 12000000 | tf_op jit(solution)/shard_map/mla_attn/pallas_call | solution.py:463
  177.2 0.0 all-to-all-done.1
  177.2 4.8 %all-to-all-start = ((bf16[8,256,512]{2,1,0:T(8,128)(2,1)}), bf16[8,256,512]{2,1,0:T(8,128)(2,1)S(1)}, u32[]{:S(2)}, u32[]{:S(2)}) async-start(bf16[8,256,512]{2,1,0:T(8,128)(2,1)} %bitcast.18), calls=%async_computation | async-start | bytes 4194304 | tf_op jit(solution)/shard_map/all_to_all | solution.py:596
  182.0 32.1 %mla_attn.6 = bf16[2048,512]{1,0:T(8,128)(2,1)} custom-call(bf16[2048,640]{1,0:T(8,128)(2,1)} %get-tuple-element.16.kv_ref, bf16[2048,1536]{1,0:T(8,128)(2,1)} %get-tuple-element.17.cq_ref, f32[512,256]{1,0:T(8,128)} %get-tuple-element.18.cs_ref, bf16[1536,2048]{1,0:T(8,128)(2,1)} %get-tuple-element.19.wn_ref, bf16[1536,1024]{1,0:T(8,128)(2,1)} %get-tuple-element.20.wr_ref, ...), custom_call_target="tpu_custom_call" | custom-call | flops 20401094656 | bytes 12000000 | tf_op jit(solution)/shard_map/mla_attn/pallas_call | solution.py:463
  214.1 0.0 all-to-all-done
  214.1 4.8 %all-to-all-start.2 = ((bf16[8,256,512]{2,1,0:T(8,128)(2,1)}), bf16[8,256,512]{2,1,0:T(8,128)(2,1)}, u32[]{:S(2)}, u32[]{:S(2)}) async-start(bf16[8,256,512]{2,1,0:T(8,128)(2,1)} %bitcast.17), calls=%async_computation.2 | async-start | bytes 4194304 | tf_op jit(solution)/shard_map/all_to_all | solution.py:596
  218.9 42.5 %out_product.2.refs_0_ = f32[256,7168]{1,0:T(8,128)} custom-call(bf16[2048,512]{1,0:T(8,128)(2,1)} %bitcast.15, bf16[2048,512]{1,0:T(8,128)(2,1)} %bitcast.7.refs_1_, bf16[8,4,512,7168]{3,2,1,0:T(8,128)(2,1)} %bitcast.8.refs_2_.refs_3_), custom_call_target="tpu_custom_call" | custom-call | flops 30064771072 | bytes 117440512 | tf_op jit(solution)/shard_map/out_product/pallas_call | solution.py:551
  261.5 0.0 all-to-all-done.2
  261.5 45.2 %out_product.3 = bf16[256,7168]{1,0:T(8,128)(2,1)} custom-call(f32[256,7168]{1,0:T(8,128)} %out_product.2.refs_0_, bf16[2048,512]{1,0:T(8,128)(2,1)} %bitcast.10.refs_1_, bf16[2048,512]{1,0:T(8,128)(2,1)} %bitcast.14, bf16[8,4,512,7168]{3,2,1,0:T(8,128)(2,1)} %bitcast.8.refs_2_.refs_3_), custom_call_target="tpu_custom_call" | custom-call | flops 30064771072 | bytes 117440512 | tf_op jit(solution)/shard_map/out_product/pallas_call | solution.py:551
  (5 shorter events, 0.0 us)
Async XLA Ops:
  103.6 4.0 %copy-start.2 = (bf16[256,64]{1,0:T(8,128)(2,1)S(1)}, bf16[256,64]{1,0:T(8,128)(2,1)}, u32[]{:S(2)}) copy-start(bf16[256,64]{1,0:T(8,128)(2,1)} %get-tuple-element.27) | copy-start | bytes 98308
  103.6 36.8 %all-to-all-start.3 = ((bf16[8,256,512]{2,1,0:T(8,128)(2,1)}), bf16[8,256,512]{2,1,0:T(8,128)(2,1)S(1)}, u32[]{:S(2)}, u32[]{:S(2)}) async-start(bf16[8,256,512]{2,1,0:T(8,128)(2,1)} %bitcast.20), calls=%async_computation.3 | async-start | bytes 4194304 | tf_op jit(solution)/shard_map/all_to_all | solution.py:596
  140.4 36.8 %copy-start = (bf16[8,256,512]{2,1,0:T(8,128)(2,1)}, bf16[8,256,512]{2,1,0:T(8,128)(2,1)S(1)}, u32[]{:S(2)}) copy-start(bf16[8,256,512]{2,1,0:T(8,128)(2,1)S(1)} %all-to-all-done.3) | copy-start | bytes 6291460
  140.4 36.7 %all-to-all-start.1 = ((bf16[8,256,512]{2,1,0:T(8,128)(2,1)}), bf16[8,256,512]{2,1,0:T(8,128)(2,1)}, u32[]{:S(2)}, u32[]{:S(2)}) async-start(bf16[8,256,512]{2,1,0:T(8,128)(2,1)} %bitcast.19), calls=%async_computation.1 | async-start | bytes 4194304 | tf_op jit(solution)/shard_map/all_to_all | solution.py:596
  177.2 36.9 %all-to-all-start = ((bf16[8,256,512]{2,1,0:T(8,128)(2,1)}), bf16[8,256,512]{2,1,0:T(8,128)(2,1)S(1)}, u32[]{:S(2)}, u32[]{:S(2)}) async-start(bf16[8,256,512]{2,1,0:T(8,128)(2,1)} %bitcast.18), calls=%async_computation | async-start | bytes 4194304 | tf_op jit(solution)/shard_map/all_to_all | solution.py:596
  214.1 4.8 %copy-start.1 = (bf16[8,256,512]{2,1,0:T(8,128)(2,1)}, bf16[8,256,512]{2,1,0:T(8,128)(2,1)S(1)}, u32[]{:S(2)}) copy-start(bf16[8,256,512]{2,1,0:T(8,128)(2,1)S(1)} %all-to-all-done) | copy-start | bytes 6291460
  214.1 47.4 %all-to-all-start.2 = ((bf16[8,256,512]{2,1,0:T(8,128)(2,1)}), bf16[8,256,512]{2,1,0:T(8,128)(2,1)}, u32[]{:S(2)}, u32[]{:S(2)}) async-start(bf16[8,256,512]{2,1,0:T(8,128)(2,1)} %bitcast.17), calls=%async_computation.2 | async-start | bytes 4194304 | tf_op jit(solution)/shard_map/all_to_all | solution.py:596

commit v4 on v3

--- a/solution.py
+++ b/solution.py
@@ -16,7 +16,7 @@
 MESH = pl.DeviceIdType.MESH
 LANES = 128
 NEG = -1e30
-GROUP = 4
+GROUP = 8
 
 
 def rope_freqs(rot_dim):
@@ -57,7 +57,7 @@
 LSLOTS = 6
 
 
-def latent_kernel(kv_rank, x_ref, wq_ref, wkvt_ref, gq_ref, gkv_ref, cos_ref, sin_ref, cq_ref, kv_ref, pe_ref, own_ref, xb, qb, kb, acc_q, acc_kv, sem):
+def latent_kernel(kv_rank, x_ref, wq_ref, wkvt_ref, gq_ref, gkv_ref, cs_ref, cq_ref, kv_ref, pe_ref, own_ref, xb, qb, kb, acc_q, acc_kv, sem):
     bf = jnp.bfloat16
     steps = x_ref.shape[1] // LK
 
@@ -93,13 +93,15 @@
     cq_ref[...] = rms_norm(acc_q[...], gq_ref[...]).astype(bf)
     lat = rms_norm(acc_kv[:, :kv_rank], gkv_ref[...]).astype(bf)
     kv_ref[...] = lat
-    pe = rotate_half(acc_kv[:, kv_rank:], cos_ref[...], sin_ref[...]).astype(bf)
+    cs = cs_ref[...].T
+    half = cs.shape[1] // 2
+    pe = rotate_half(acc_kv[:, kv_rank:], cs[:, :half], cs[:, half:]).astype(bf)
     pe_ref[...] = pe
     own_ref[:, :kv_rank] = lat
     own_ref[:, kv_rank:] = jnp.concatenate([pe, jnp.zeros((pe.shape[0], LANES - pe.shape[1]), bf)], axis=1)
 
 
-def latents(x, w_dq, w_dkv, g_q, g_kv, cos_t, sin_t):
+def latents(x, w_dq, w_dkv, g_q, g_kv, cs_own):
     rows, hidden = x.shape
     rank = w_dq.shape[1]
     kvw = w_dkv.shape[1]
@@ -110,7 +112,7 @@
     vm = pl.BlockSpec(memory_space=pltpu.VMEM)
     return pl.pallas_call(
         functools.partial(latent_kernel, kv_rank),
-        in_specs=[anyspec] * 3 + [vm] * 4,
+        in_specs=[anyspec] * 3 + [vm] * 3,
         out_specs=[vm] * 4,
         out_shape=[
             jax.ShapeDtypeStruct((rows, rank), bf),
@@ -129,7 +131,7 @@
         compiler_params=pltpu.CompilerParams(vmem_limit_bytes=60_000_000),
         cost_estimate=pl.CostEstimate(flops=2 * rows * hidden * (rank + kvw), bytes_accessed=2 * hidden * (rank + kvw + rows), transcendentals=0),
         name="latents",
-    )(x, w_dq, w_dkv.T, g_q[None, :], g_kv[None, :], cos_t, sin_t)
+    )(x, w_dq, w_dkv.T, g_q[None, :], g_kv[None, :], cs_own)
 
 
 SUB = 16
@@ -412,13 +414,19 @@
 
     def soft_diag(h, slot):
         m = mxb[slot][...]
-        pa = jnp.exp2((sbuf[slot][:hb, :] - m) * scale2)
-        pb = jnp.exp2((sbuf[slot][hb:, hb:] - m[:, hb:]) * scale2)
-        pbuf[slot][:hb, :] = pa.astype(bf)
-        pbuf[slot][hb:, hb:] = pb.astype(bf)
-        la = jnp.sum(pa, axis=0, keepdims=True)
-        lrow[h, :, :hb] = la[:, :hb]
-        lrow[h, :, hb:] = la[:, hb:] + jnp.sum(pb, axis=0, keepdims=True)
+        ta = tb = None
+        for c in range(0, hb, CH):
+            pa = jnp.exp2((sbuf[slot][c:c + CH, :] - m) * scale2)
+            pbuf[slot][c:c + CH, :] = pa.astype(bf)
+            part = jnp.sum(pa.reshape(CH // 8, 8, QB), axis=0)
+            ta = part if ta is None else ta + part
+        for c in range(hb, QB, CH):
+            pb = jnp.exp2((sbuf[slot][c:c + CH, hb:] - m[:, hb:]) * scale2)
+            pbuf[slot][c:c + CH, hb:] = pb.astype(bf)
+            part = jnp.sum(pb.reshape(CH // 8, 8, hb), axis=0)
+            tb = part if tb is None else tb + part
+        lrow[h, :, :hb] = jnp.sum(ta[:, :hb], axis=0, keepdims=True)
+        lrow[h, :, hb:] = jnp.sum(ta[:, hb:] + tb, axis=0, keepdims=True)
         mrow[h] = m
 
     def weigh_diag(h, slot):
@@ -495,28 +503,29 @@
 
 
 OSLOTS = 3
-NT = 1024
+NT = 512
+NH = 2
 
 
 def out_kernel(n, call, first, *refs):
     if first:
-        oa, ob, w_ref, out_ref, wbuf, acc, sem, acc_sem = refs
+        o_ref, w_ref, out_ref, wbuf, acc, sem, acc_sem = refs
     else:
-        acc_in, oa, ob, w_ref, out_ref, wbuf, acc, sem, acc_sem = refs
-    rows = oa.shape[0] // n
+        acc_in, o_ref, w_ref, out_ref, wbuf, acc, prev, sem, acc_sem = refs
+    rows = o_ref.shape[0] // n
     hidden = w_ref.shape[3]
-    steps = 2 * n
+    wide = hidden // NH
+    steps = NH * n
 
     def copy(s, slot):
-        return pltpu.make_async_copy(w_ref.at[lax.rem(s, n), 2 * call + s // n], wbuf.at[slot], sem.at[slot])
+        cols = pl.ds(pl.multiple_of(lax.rem(s, NH) * wide, LANES), wide)
+        return pltpu.make_async_copy(w_ref.at[s // NH, call, :, cols], wbuf.at[slot], sem.at[slot])
 
     for s in range(OSLOTS - 1):
         copy(s, s).start()
-    if first:
-        acc[...] = jnp.zeros_like(acc)
-    else:
-        pltpu.make_async_copy(acc_in, acc, acc_sem).start()
-        pltpu.make_async_copy(acc_in, acc, acc_sem).wait()
+    if not first:
+        pltpu.make_async_copy(acc_in, prev, acc_sem).start()
+    acc[...] = jnp.zeros_like(acc)
 
     def body(s, _):
         slot = lax.rem(s, OSLOTS)
@@ -525,11 +534,11 @@
         def _():
             copy(s + OSLOTS - 1, lax.rem(s + OSLOTS - 1, OSLOTS)).start()
         copy(s, slot).wait()
-        r = pl.ds(pl.multiple_of(lax.rem(s, n) * rows, rows), rows)
-        lhs = jnp.where(s < n, oa[r, :], ob[r, :])
-        for t in range(hidden // NT):
+        lhs = o_ref[pl.ds(pl.multiple_of((s // NH) * rows, rows), rows), :]
+        side = lax.rem(s, NH)
+        for t in range(wide // NT):
             cols = slice(t * NT, (t + 1) * NT)
-            acc[:, cols] += dot_nn(lhs, wbuf[slot, :, cols])
+            acc[side, :, cols] += dot_nn(lhs, wbuf[slot, :, cols])
         return 0
 
     lax.fori_loop(0, steps, body, 0)
@@ -537,30 +546,34 @@
         pltpu.make_async_copy(acc, out_ref, acc_sem).start()
         pltpu.make_async_copy(acc, out_ref, acc_sem).wait()
     else:
-        out_ref[...] = acc[...].astype(out_ref.dtype)
-
-
-def out_product(acc, oa, ob, w4, call, n):
-    seq, width = oa.shape
+        pltpu.make_async_copy(acc_in, prev, acc_sem).wait()
+        for i in range(NH):
+            out_ref[:, i * wide:(i + 1) * wide] = (prev[i] + acc[i]).astype(out_ref.dtype)
+
+
+def out_product(acc, o, w4, call, n):
+    seq, width = o.shape
     rows = seq // n
     hidden = w4.shape[3]
     first = acc is None
     anyspec = pl.BlockSpec(memory_space=pl.ANY)
     vm = pl.BlockSpec(memory_space=pltpu.VMEM)
-    args = ([] if first else [acc]) + [oa, ob, w4]
+    args = ([] if first else [acc]) + [o, w4]
+    sums = pltpu.VMEM((NH, rows, hidden // NH), jnp.float32)
     return pl.pallas_call(
         functools.partial(out_kernel, n, call, first),
-        in_specs=([] if first else [anyspec]) + [vm, vm, anyspec],
+        in_specs=([] if first else [anyspec]) + [vm, anyspec],
         out_specs=anyspec if first else vm,
-        out_shape=jax.ShapeDtypeStruct((rows, hidden), jnp.float32 if first else jnp.bfloat16),
+        out_shape=jax.ShapeDtypeStruct((NH, rows, hidden // NH), jnp.float32) if first else jax.ShapeDtypeStruct((rows, hidden), jnp.bfloat16),
         scratch_shapes=[
-            pltpu.VMEM((OSLOTS, width, hidden), jnp.bfloat16),
-            pltpu.VMEM((rows, hidden), jnp.float32),
+            pltpu.VMEM((OSLOTS, width, hidden // NH), jnp.bfloat16),
+            sums,
+        ] + ([] if first else [sums]) + [
             pltpu.SemaphoreType.DMA((OSLOTS,)),
             pltpu.SemaphoreType.DMA,
         ],
         compiler_params=pltpu.CompilerParams(vmem_limit_bytes=60_000_000),
-        cost_estimate=pl.CostEstimate(flops=4 * rows * hidden * width * n, bytes_accessed=4 * hidden * width * n, transcendentals=0),
+        cost_estimate=pl.CostEstimate(flops=2 * rows * hidden * width * n, bytes_accessed=2 * hidden * width * n, transcendentals=0),
         name="out_product",
     )(*args)
 
@@ -581,10 +594,9 @@
         vd = w_uv.shape[2]
         scale2 = (0.1 * math.log(YARN_FACTOR) + 1.0) ** 2 / math.sqrt(qk_dim) / math.log(2.0)
 
-        angles = tok_pos.astype(jnp.float32)[:, None] * rope_freqs(rot)[None, :]
-        cos_t, sin_t = jnp.cos(angles), jnp.sin(angles)
-        cs_own = jnp.concatenate([cos_t, sin_t], axis=1).T
-        cq_own, cache_kv, cache_pe, kv_own = latents(tok_in, w_dq, w_dkv, g_q, g_kv, cos_t, sin_t)
+        angles = rope_freqs(rot)[:, None] * tok_pos.astype(jnp.float32)[None, :]
+        cs_own = jnp.concatenate([jnp.cos(angles), jnp.sin(angles)], axis=0)
+        cq_own, cache_kv, cache_pe, kv_own = latents(tok_in, w_dq, w_dkv, g_q, g_kv, cs_own)
 
         w_t = jnp.transpose(w_uq, (0, 2, 1))
         kv_all, cs_all, cq_all, wn, wr, uk, uv = gather_and_pick(n, heads, nope, kv_own, cs_own, cq_own, w_t, w_uk, w_uv)
@@ -596,8 +608,8 @@
             o_parts.append(lax.all_to_all(o_g, 'sp', 0, 0, tiled=True))
         w4 = w_o.reshape(n, chunks, GROUP * vd, w_o.shape[2])
         acc = None
-        for call in range(chunks // 2):
-            acc = out_product(acc, o_parts[2 * call], o_parts[2 * call + 1], w4, call, n)
+        for call in range(chunks):
+            acc = out_product(acc, o_parts[call], w4, call, n)
         return acc, cache_kv, cache_pe
 
     return jax.shard_map(local_step, mesh=mesh, in_specs=(rows_spec, tok_spec, rep, rep, rep, rep, rep, rep, rep, rep), out_specs=(rows_spec, rows_spec, rows_spec), check_vma=False)

time: 307 us -> 279 us (0.909)
  Pallas kernels: 282 us -> 258 us
  starting transfers between devices: 18.3 us -> 9.9 us
  waiting for transfers between devices: 0.01 us -> 5.82 us
    pallas_call x4 -> x2, Pallas kernels: 128 us -> 106 us  [attention_group(): pl.pallas_call(functools.partial(attn_kernel, scale2, kv_rank, nope, rot)...]
    all_to_all x4 -> x2, starting transfers between devices: 18.3 us -> 9.9 us  [local_step(): o_parts.append(lax.all_to_all(o_g, 'sp', 0, 0, tiled=True))]
    all_to_all x4 -> x2, waiting for transfers between devices: 0.01 us -> 5.82 us  [local_step(): o_parts.append(lax.all_to_all(o_g, 'sp', 0, 0, tiled=True))]
  transfers between devices with their start and end apart: 4 -> 2, of which waited for: 0 -> 1; matrix products, arithmetic and copies ran while one was open for 0% -> 0% of each run, Pallas kernels for 45% -> 34%
where the time goes in v4:
time: 279 us
  Pallas kernels  258 us (92%)
  starting transfers between devices  9.9 us (4%)
  waiting for transfers between devices  5.82 us (2%)
    pallas_call x2, Pallas kernels, attention_group(): pl.pallas_call(functools.partial(attn_kernel, scale2, kv_rank, nope, rot)...  106 us
    pallas_call x2, Pallas kernels, out_product(): pl.pallas_call(functools.partial(out_kernel, n, call, first), in_specs=([...  86 us
    pallas_call x1, Pallas kernels, gather_and_pick(): pl.pallas_call(functools.partial(gather_kernel, n, heads, nope), grid=(st...  50.7 us
    pallas_call x1, Pallas kernels, latents(): pl.pallas_call(functools.partial(latent_kernel, kv_rank), in_specs=[anysp...  15.1 us
    all_to_all x2, starting transfers between devices, local_step(): o_parts.append(lax.all_to_all(o_g, 'sp', 0, 0, tiled=True))  9.9 us
    all_to_all x2, waiting for transfers between devices, local_step(): o_parts.append(lax.all_to_all(o_g, 'sp', 0, 0, tiled=True))  5.82 us
  transfers between devices with their start and end apart: 2, of which 1 were waited for; matrix products, arithmetic and copies ran while one was open for 0% of the time, Pallas kernels for 34%

profile of v4, /device:TPU:81, one launch (start us, length us, event | category | flops | bytes accessed | tf_op | source)
XLA Modules:
  0.0 278.8 jit_solution(5902058055788622205)
XLA Ops:
  0.6 0.7 convert_element_type.3
  1.3 1.3 broadcast_in_dim.8.gq_ref
  2.6 0.9 multiply_cosine_fusion
  3.5 0.6 pad_maximum_fusion.cs_ref
  4.1 15.1 %latents.1 = (bf16[256,1536]{1,0:T(8,128)(2,1)}, bf16[256,512]{1,0:T(8,128)(2,1)}, bf16[256,64]{1,0:T(8,128)(2,1)}, bf16[256,640]{1,0:T(8,128)(2,1)}) custom-call(bf16[256,7168]{1,0:T(8,128)(2,1)} %x_ref.1, bf16[7168,1536]{1,0:T(8,128)(2,1)} %wq_ref.1, bf16[576,7168]{1,0:T(8,128)(2,1)} %bitcast.8, f32[1,1536]{1,0:T(1,128)} %broadcast_in_dim.8.gq_ref, ...), custom_call_target="tpu_custom_call" | custom-call | flops 7751073792 | bytes 33947648 | tf_op jit(solution)/shard_map/latents/pallas_call | solution.py:113
  19.2 50.7 %gather_pick.1 = (bf16[2048,640]{1,0:T(8,128)(2,1)}, f32[512,256]{1,0:T(8,128)}, bf16[2048,1536]{1,0:T(8,128)(2,1)}, bf16[1536,2048]{1,0:T(8,128)(2,1)}, bf16[15...) custom-call(bf16[256,640]{1,0:T(8,128)(2,1)} %get-tuple-element.14.kv_ref, ...), custom_call_target="tpu_custom_call" | custom-call | flops 30000001024 | bytes 90000000 | tf_op jit(solution)/shard_map/gather_pick/pallas_call | solution.py:281
  69.9 53.2 %mla_attn.2 = bf16[2048,1024]{1,0:T(8,128)(2,1)} custom-call(bf16[2048,640]{1,0:T(8,128)(2,1)} %get-tuple-element.16.kv_ref, bf16[2048,1536]{1,0:T(8,128)(2,1)} %get-tuple-element.17.cq_ref, f32[512,256]{1,0:T(8,128)} %get-tuple-element.18.cs_ref, bf16[1536,2048]{1,0:T(8,128)(2,1)} %get-tuple-element.19.wn_ref, bf16[1536,1024]{1,0:T(8,128)(2,1)} %get-tuple-element.20.wr_ref, ...), custom_call_target="tpu_custom_call" | custom-call | flops 40802189312 | bytes 12000000 | tf_op jit(solution)/shard_map/mla_attn/pallas_call | solution.py:471
  123.2 4.9 %all-to-all-start = ((bf16[8,256,1024]{2,1,0:T(8,128)(2,1)}), bf16[8,256,1024]{2,1,0:T(8,128)(2,1)}, u32[]{:S(2)}, u32[]{:S(2)}) async-start(bf16[8,256,1024]{2,1,0:T(8,128)(2,1)} %bitcast.10), calls=%async_computation | async-start | bytes 8388608 | tf_op jit(solution)/shard_map/all_to_all | solution.py:608
  128.0 52.9 %mla_attn.3 = bf16[2048,1024]{1,0:T(8,128)(2,1)} custom-call(bf16[2048,640]{1,0:T(8,128)(2,1)} %get-tuple-element.16.kv_ref, bf16[2048,1536]{1,0:T(8,128)(2,1)} %get-tuple-element.17.cq_ref, f32[512,256]{1,0:T(8,128)} %get-tuple-element.18.cs_ref, bf16[1536,2048]{1,0:T(8,128)(2,1)} %get-tuple-element.19.wn_ref, bf16[1536,1024]{1,0:T(8,128)(2,1)} %get-tuple-element.20.wr_ref, ...), custom_call_target="tpu_custom_call" | custom-call | flops 40802189312 | bytes 12000000 | tf_op jit(solution)/shard_map/mla_attn/pallas_call | solution.py:471
  180.9 0.0 all-to-all-done
  180.9 0.0 copy-start
  180.9 5.0 %all-to-all-start.1 = ((bf16[8,256,1024]{2,1,0:T(8,128)(2,1)}), bf16[8,256,1024]{2,1,0:T(8,128)(2,1)}, u32[]{:S(2)}, u32[]{:S(2)}) async-start(bf16[8,256,1024]{2,1,0:T(8,128)(2,1)} %bitcast.9), calls=%async_computation.1 | async-start | bytes 8388608 | tf_op jit(solution)/shard_map/all_to_all | solution.py:608
  186.0 0.0 copy-done
  186.0 0.7 copy.14
  186.7 41.9 %out_product.2.refs_0_ = f32[2,256,3584]{2,1,0:T(8,128)} custom-call(bf16[2048,1024]{1,0:T(8,128)(2,1)} %bitcast.4.refs_0_, bf16[8,2,1024,7168]{3,2,1,0:T(8,128)(2,1)} %bitcast.5.refs_1_.refs_2_), custom_call_target="tpu_custom_call" | custom-call | flops 30064771072 | bytes 117440512 | tf_op jit(solution)/shard_map/out_product/pallas_call | solution.py:563
  228.7 5.8 %all-to-all-done.1 = bf16[8,256,1024]{2,1,0:T(8,128)(2,1)} async-done(((bf16[8,256,1024]{2,1,0:T(8,128)(2,1)}), bf16[8,256,1024]{2,1,0:T(8,128)(2,1)}, u32[]{:S(2)}, u32[]{:S(2)}) %all-to-all-start.1) | async-done | bytes 4194336 | tf_op jit(solution)/shard_map/all_to_all | solution.py:608
  234.5 44.1 %out_product.3 = bf16[256,7168]{1,0:T(8,128)(2,1)} custom-call(f32[2,256,3584]{2,1,0:T(8,128)} %out_product.2.refs_0_, bf16[2048,1024]{1,0:T(8,128)(2,1)} %bitcast.7.refs_1_, bf16[8,2,1024,7168]{3,2,1,0:T(8,128)(2,1)} %bitcast.5.refs_1_.refs_2_), custom_call_target="tpu_custom_call" | custom-call | flops 30064771072 | bytes 117440512 | tf_op jit(solution)/shard_map/out_product/pallas_call | solution.py:563
Async XLA Ops:
  123.2 57.8 %all-to-all-start = ((bf16[8,256,1024]{2,1,0:T(8,128)(2,1)}), bf16[8,256,1024]{2,1,0:T(8,128)(2,1)}, u32[]{:S(2)}, u32[]{:S(2)}) async-start(bf16[8,256,1024]{2,1,0:T(8,128)(2,1)} %bitcast.10), calls=%async_computation | async-start | bytes 8388608 | tf_op jit(solution)/shard_map/all_to_all | solution.py:608
  180.9 5.1 %copy-start = (bf16[256,64]{1,0:T(8,128)(2,1)S(1)}, bf16[256,64]{1,0:T(8,128)(2,1)}, u32[]{:S(2)}) copy-start(bf16[256,64]{1,0:T(8,128)(2,1)} %get-tuple-element.27) | copy-start | bytes 98308
  180.9 53.5 %all-to-all-start.1 = ((bf16[8,256,1024]{2,1,0:T(8,128)(2,1)}), bf16[8,256,1024]{2,1,0:T(8,128)(2,1)}, u32[]{:S(2)}, u32[]{:S(2)}) async-start(bf16[8,256,1024]{2,1,0:T(8,128)(2,1)} %bitcast.9), calls=%async_computation.1 | async-start | bytes 8388608 | tf_op jit(solution)/shard_map/all_to_all | solution.py:608

commit v5 on v4

--- a/solution.py
+++ b/solution.py
@@ -53,8 +53,8 @@
     return jnp.dot(a, b, preferred_element_type=jnp.float32)
 
 
-LK = 512
-LSLOTS = 6
+LK = 1024
+LSLOTS = 4
 
 
 def latent_kernel(kv_rank, x_ref, wq_ref, wkvt_ref, gq_ref, gkv_ref, cs_ref, cq_ref, kv_ref, pe_ref, own_ref, xb, qb, kb, acc_q, acc_kv, sem):
@@ -90,8 +90,8 @@
         return 0
 
     lax.fori_loop(0, steps, body, 0)
-    cq_ref[...] = rms_norm(acc_q[...], gq_ref[...]).astype(bf)
-    lat = rms_norm(acc_kv[:, :kv_rank], gkv_ref[...]).astype(bf)
+    cq_ref[...] = rms_norm(acc_q[...], gq_ref[...].reshape(1, -1)).astype(bf)
+    lat = rms_norm(acc_kv[:, :kv_rank], gkv_ref[...].reshape(1, -1)).astype(bf)
     kv_ref[...] = lat
     cs = cs_ref[...].T
     half = cs.shape[1] // 2
@@ -131,11 +131,11 @@
         compiler_params=pltpu.CompilerParams(vmem_limit_bytes=60_000_000),
         cost_estimate=pl.CostEstimate(flops=2 * rows * hidden * (rank + kvw), bytes_accessed=2 * hidden * (rank + kvw + rows), transcendentals=0),
         name="latents",
-    )(x, w_dq, w_dkv.T, g_q[None, :], g_kv[None, :], cs_own)
+    )(x, w_dq, w_dkv.T, g_q, g_kv, cs_own)
 
 
 SUB = 16
-CBLK = 192
+CBLK = 96
 
 
 def gather_kernel(n, heads, nope, kv_ref, cs_ref, cq_ref, wt_ref, uk_ref, uv_ref, kv_all, cs_all, cq_all, wn_ref, wr_ref, uko_ref, uvo_ref, sel, tn, tr, tu, send_sem, recv_sem, loc_sem):
@@ -219,17 +219,22 @@
         cps[arr][3].wait_recv()
         cps[arr][8].start()
 
-    @pl.when(step == (3 * last) // 7)
+    @pl.when(step == (5 * last) // 15)
     def _():
         hand_on(2)
 
-    @pl.when(step == (5 * last) // 7)
+    @pl.when(step == (8 * last) // 15)
     def _():
         to_mate(2)
 
-    @pl.when(step == last)
+    @pl.when(step == (10 * last) // 15)
     def _():
         hand_on(0)
+
+    @pl.when(step == (12 * last) // 15)
+    def _():
+        hand_on(1)
+        to_mate(0)
 
     for s in range(CBLK // SUB):
         lhs = jnp.concatenate([wt_ref[s * SUB + i] for i in range(SUB)], axis=1)
@@ -251,8 +256,6 @@
 
     @pl.when(step == last)
     def _():
-        hand_on(1)
-        to_mate(0)
         to_mate(1)
         for arr in (2, 0, 1):
             cps[arr][5].wait_recv()
@@ -326,7 +329,7 @@
 CH = 16
 
 
-def attn_kernel(scale2, kv_rank, nope, rot, kv_ref, cq_ref, cs_ref, wn_ref, wr_ref, uk_ref, uv_ref, o_ref, kcat, vt, uvt, qcat, acc, mrow, lrow, s0, s1, p0, p1, mx0, mx1, al0, al1):
+def attn_kernel(g, scale2, kv_rank, nope, rot, kv_ref, cq_ref, cs_ref, wn_hbm, wr_hbm, uk_ref, uv_ref, o_ref, wn_ref, wr_ref, wsem, kcat, vt, uvt, qcat, acc, mrow, lrow, s0, s1, p0, p1, mx0, mx1, al0, al1):
     b = pl.program_id(0)
     vd = uv_ref.shape[1] // GROUP
     bf = jnp.bfloat16
@@ -336,6 +339,12 @@
 
     @pl.when(b == 0)
     def _():
+        loads = [
+            pltpu.make_async_copy(src.at[:, pl.ds(g * dst.shape[1], dst.shape[1])], dst, wsem.at[i])
+            for i, (src, dst) in enumerate(((wn_hbm, wn_ref), (wr_hbm, wr_ref)))
+        ]
+        for c in loads:
+            c.start()
         uvt[...] = uv_ref[...].T
 
         def fill(i, _):
@@ -350,6 +359,8 @@
             vt[:, r] = dot_nt(uvt[...], c).astype(bf)
             return 0
         lax.fori_loop(0, kv_ref.shape[0] // QB, fill, 0)
+        for c in loads:
+            c.wait()
 
     cq = cq_ref[...]
     qn = dot_nn(cq, wn_ref[...]).astype(bf)
@@ -377,9 +388,13 @@
     tri = lax.broadcasted_iota(jnp.int32, (hb, hb), 0) <= lax.broadcasted_iota(jnp.int32, (hb, hb), 1)
 
     def score(h, r, slot):
-        s = dot_nt(kcat[h, pl.ds(r, QB), :], qcat[h])
-        sbuf[slot][...] = s
-        mxb[slot][...] = jnp.max(s, axis=0, keepdims=True)
+        m = None
+        for c in (0, hb):
+            s = dot_nt(kcat[h, pl.ds(r + c, hb), :], qcat[h])
+            sbuf[slot][c:c + hb, :] = s
+            mc = jnp.max(s, axis=0, keepdims=True)
+            m = mc if m is None else jnp.maximum(m, mc)
+        mxb[slot][...] = m
 
     def soft(h, slot):
         m_old = mrow[h]
@@ -469,20 +484,23 @@
     flops = 2 * GROUP * (seq * rank * (nope + rot) + seq * kv_rank * (nope + vd) + pairs * (nope + rot + vd) * 2)
     row = pltpu.VMEM((1, QB), f32)
     return pl.pallas_call(
-        functools.partial(attn_kernel, scale2, kv_rank, nope, rot),
+        functools.partial(attn_kernel, g, scale2, kv_rank, nope, rot),
         grid=(blocks,),
         in_specs=[
             pl.BlockSpec(kv_all.shape, lambda b: (0, 0)),
             pl.BlockSpec((QB, rank), lambda b: (b, 0)),
             pl.BlockSpec((cs_all.shape[0] // blocks, cs_all.shape[1]), lambda b: (b, 0)),
-            pl.BlockSpec((rank, GROUP * nope), lambda b: (0, g)),
-            pl.BlockSpec((rank, GROUP * rot), lambda b: (0, g)),
+            pl.BlockSpec(memory_space=pl.ANY),
+            pl.BlockSpec(memory_space=pl.ANY),
             pl.BlockSpec((kv_rank, GROUP * nope), lambda b: (0, g)),
             pl.BlockSpec((kv_rank, GROUP * vd), lambda b: (0, g)),
         ],
         out_specs=pl.BlockSpec((QB, GROUP * vd), lambda b: (b, 0)),
         out_shape=jax.ShapeDtypeStruct((seq, GROUP * vd), bf),
         scratch_shapes=[
+            pltpu.VMEM((rank, GROUP * nope), bf),
+            pltpu.VMEM((rank, GROUP * rot), bf),
+            pltpu.SemaphoreType.DMA((2,)),
             pltpu.VMEM((GROUP, seq, nope + LANES), bf),
             pltpu.VMEM((GROUP * vd, seq), bf),
             pltpu.VMEM((GROUP * vd, kv_rank), bf),

time: 279 us -> 271 us (0.971)
  Pallas kernels: 258 us -> 251 us
    pallas_call x2, Pallas kernels: 106 us -> 101 us  [attention_group(): pl.pallas_call(functools.partial(attn_kernel, g, scale2, kv_rank, nope, r...]
where the time goes in v5:
time: 271 us
  Pallas kernels  251 us (93%)
  starting transfers between devices  9.91 us (4%)
  waiting for transfers between devices  5.84 us (2%)
    pallas_call x2, Pallas kernels, attention_group(): pl.pallas_call(functools.partial(attn_kernel, g, scale2, kv_rank, nope, r...  101 us
    pallas_call x2, Pallas kernels, out_product(): pl.pallas_call(functools.partial(out_kernel, n, call, first), in_specs=([...  86 us
    pallas_call x1, Pallas kernels, gather_and_pick(): pl.pallas_call(functools.partial(gather_kernel, n, heads, nope), grid=(st...  49.1 us
    pallas_call x1, Pallas kernels, latents(): pl.pallas_call(functools.partial(latent_kernel, kv_rank), in_specs=[anysp...  14.7 us
    all_to_all x2, starting transfers between devices, local_step(): o_parts.append(lax.all_to_all(o_g, 'sp', 0, 0, tiled=True))  9.91 us
    all_to_all x2, waiting for transfers between devices, local_step(): o_parts.append(lax.all_to_all(o_g, 'sp', 0, 0, tiled=True))  5.84 us
  transfers between devices with their start and end apart: 2, of which 1 were waited for; matrix products, arithmetic and copies ran while one was open for 0% of the time, Pallas kernels for 34%

profile of v5, /device:TPU:81, one launch (start us, length us, event | category | flops | bytes accessed | tf_op | source)
XLA Modules:
  0.0 270.6 jit_solution(5149415308116469663)
XLA Ops:
  0.6 0.7 convert_element_type.3
  1.3 0.9 multiply_cosine_fusion
  2.2 0.6 pad_maximum_fusion.cs_ref
  2.8 14.7 %latents.1 = (bf16[256,1536]{1,0:T(8,128)(2,1)}, bf16[256,512]{1,0:T(8,128)(2,1)}, bf16[256,64]{1,0:T(8,128)(2,1)}, bf16[256,640]{1,0:T(8,128)(2,1)}) custom-call(bf16[256,7168]{1,0:T(8,128)(2,1)} %x_ref.1, bf16[7168,1536]{1,0:T(8,128)(2,1)} %wq_ref.1, bf16[576,7168]{1,0:T(8,128)(2,1)} %bitcast.7, f32[1536]{0:T(1024)} %gq_ref.1, f32[512]{0:T(512)} %gkv_ref.1, ...), custom_call_target="tpu_custom_call" | custom-call | flops 7751073792 | bytes 33947648 | tf_op jit(solution)/shard_map/latents/pallas_call | solution.py:113
  17.5 49.1 %gather_pick.1 = (bf16[2048,640]{1,0:T(8,128)(2,1)}, f32[512,256]{1,0:T(8,128)}, bf16[2048,1536]{1,0:T(8,128)(2,1)}, bf16[1536,2048]{1,0:T(8,128)(2,1)}, bf16[15...) custom-call(bf16[256,640]{1,0:T(8,128)(2,1)} %get-tuple-element.14.kv_ref, ...), custom_call_target="tpu_custom_call" | custom-call | flops 30000001024 | bytes 90000000 | tf_op jit(solution)/shard_map/gather_pick/pallas_call | solution.py:284
  66.6 50.7 %mla_attn.2 = bf16[2048,1024]{1,0:T(8,128)(2,1)} custom-call(bf16[2048,640]{1,0:T(8,128)(2,1)} %get-tuple-element.16.kv_ref, bf16[2048,1536]{1,0:T(8,128)(2,1)} %get-tuple-element.17.cq_ref, f32[512,256]{1,0:T(8,128)} %get-tuple-element.18.cs_ref, bf16[1536,2048]{1,0:T(8,128)(2,1)} %get-tuple-element.19.wn_hbm, bf16[1536,1024]{1,0:T(8,128)(2,1)} %get-tuple-element.20.wr_hbm, ...), custom_call_target="tpu_custom_call" | custom-call | flops 40802189312 | bytes 12000000 | tf_op jit(solution)/shard_map/mla_attn/pallas_call | solution.py:486
  117.4 4.9 %all-to-all-start = ((bf16[8,256,1024]{2,1,0:T(8,128)(2,1)}), bf16[8,256,1024]{2,1,0:T(8,128)(2,1)}, u32[]{:S(2)}, u32[]{:S(2)}) async-start(bf16[8,256,1024]{2,1,0:T(8,128)(2,1)} %bitcast.9), calls=%async_computation | async-start | bytes 8388608 | tf_op jit(solution)/shard_map/all_to_all | solution.py:626
  122.3 50.5 %mla_attn.3 = bf16[2048,1024]{1,0:T(8,128)(2,1)} custom-call(bf16[2048,640]{1,0:T(8,128)(2,1)} %get-tuple-element.16.kv_ref, bf16[2048,1536]{1,0:T(8,128)(2,1)} %get-tuple-element.17.cq_ref, f32[512,256]{1,0:T(8,128)} %get-tuple-element.18.cs_ref, bf16[1536,2048]{1,0:T(8,128)(2,1)} %get-tuple-element.19.wn_hbm, bf16[1536,1024]{1,0:T(8,128)(2,1)} %get-tuple-element.20.wr_hbm, ...), custom_call_target="tpu_custom_call" | custom-call | flops 40802189312 | bytes 12000000 | tf_op jit(solution)/shard_map/mla_attn/pallas_call | solution.py:486
  172.8 0.0 all-to-all-done
  172.8 0.0 copy-start
  172.8 5.0 %all-to-all-start.1 = ((bf16[8,256,1024]{2,1,0:T(8,128)(2,1)}), bf16[8,256,1024]{2,1,0:T(8,128)(2,1)}, u32[]{:S(2)}, u32[]{:S(2)}) async-start(bf16[8,256,1024]{2,1,0:T(8,128)(2,1)} %bitcast.8), calls=%async_computation.1 | async-start | bytes 8388608 | tf_op jit(solution)/shard_map/all_to_all | solution.py:626
  177.9 0.0 copy-done
  177.9 0.7 copy.14
  178.6 41.9 %out_product.2.refs_0_ = f32[2,256,3584]{2,1,0:T(8,128)} custom-call(bf16[2048,1024]{1,0:T(8,128)(2,1)} %bitcast.3.refs_0_, bf16[8,2,1024,7168]{3,2,1,0:T(8,128)(2,1)} %bitcast.4.refs_1_.refs_2_), custom_call_target="tpu_custom_call" | custom-call | flops 30064771072 | bytes 117440512 | tf_op jit(solution)/shard_map/out_product/pallas_call | solution.py:581
  220.5 5.8 %all-to-all-done.1 = bf16[8,256,1024]{2,1,0:T(8,128)(2,1)} async-done(((bf16[8,256,1024]{2,1,0:T(8,128)(2,1)}), bf16[8,256,1024]{2,1,0:T(8,128)(2,1)}, u32[]{:S(2)}, u32[]{:S(2)}) %all-to-all-start.1) | async-done | bytes 4194336 | tf_op jit(solution)/shard_map/all_to_all | solution.py:626
  226.3 44.1 %out_product.3 = bf16[256,7168]{1,0:T(8,128)(2,1)} custom-call(f32[2,256,3584]{2,1,0:T(8,128)} %out_product.2.refs_0_, bf16[2048,1024]{1,0:T(8,128)(2,1)} %bitcast.6.refs_1_, bf16[8,2,1024,7168]{3,2,1,0:T(8,128)(2,1)} %bitcast.4.refs_1_.refs_2_), custom_call_target="tpu_custom_call" | custom-call | flops 30064771072 | bytes 117440512 | tf_op jit(solution)/shard_map/out_product/pallas_call | solution.py:581
Async XLA Ops:
  117.4 55.4 %all-to-all-start = ((bf16[8,256,1024]{2,1,0:T(8,128)(2,1)}), bf16[8,256,1024]{2,1,0:T(8,128)(2,1)}, u32[]{:S(2)}, u32[]{:S(2)}) async-start(bf16[8,256,1024]{2,1,0:T(8,128)(2,1)} %bitcast.9), calls=%async_computation | async-start | bytes 8388608 | tf_op jit(solution)/shard_map/all_to_all | solution.py:626
  172.8 5.1 %copy-start = (bf16[256,64]{1,0:T(8,128)(2,1)S(1)}, bf16[256,64]{1,0:T(8,128)(2,1)}, u32[]{:S(2)}) copy-start(bf16[256,64]{1,0:T(8,128)(2,1)} %get-tuple-element.27) | copy-start | bytes 98308
  172.8 53.5 %all-to-all-start.1 = ((bf16[8,256,1024]{2,1,0:T(8,128)(2,1)}), bf16[8,256,1024]{2,1,0:T(8,128)(2,1)}, u32[]{:S(2)}, u32[]{:S(2)}) async-start(bf16[8,256,1024]{2,1,0:T(8,128)(2,1)} %bitcast.8), calls=%async_computation.1 | async-start | bytes 8388608 | tf_op jit(solution)/shard_map/all_to_all | solution.py:626

commit v6 on v5

--- a/solution.py
+++ b/solution.py
@@ -520,9 +520,9 @@
     )(kv_all, cq_all, cs_all, wn, wr, uk, uv)
 
 
-OSLOTS = 3
+OSLOTS = 6
 NT = 512
-NH = 2
+NH = 4
 
 
 def out_kernel(n, call, first, *refs):
@@ -554,8 +554,8 @@
         copy(s, slot).wait()
         lhs = o_ref[pl.ds(pl.multiple_of((s // NH) * rows, rows), rows), :]
         side = lax.rem(s, NH)
-        for t in range(wide // NT):
-            cols = slice(t * NT, (t + 1) * NT)
+        for t in range(0, wide, NT):
+            cols = slice(t, min(t + NT, wide))
             acc[side, :, cols] += dot_nn(lhs, wbuf[slot, :, cols])
         return 0
 

time: 271 us -> 272 us (level)
  Pallas kernels: 251 us -> 254 us
  transfers between devices with their start and end apart: 2 -> 2, of which waited for: 1 -> 1; matrix products, arithmetic and copies ran while one was open for 0% -> 0% of each run, Pallas kernels for 34% -> 35%
where the time goes in v6:
time: 272 us
  Pallas kernels  254 us (93%)
  starting transfers between devices  9.91 us (4%)
  waiting for transfers between devices  4.16 us (2%)
    pallas_call x2, Pallas kernels, attention_group(): pl.pallas_call(functools.partial(attn_kernel, g, scale2, kv_rank, nope, r...  101 us
    pallas_call x2, Pallas kernels, out_product(): pl.pallas_call(functools.partial(out_kernel, n, call, first), in_specs=([...  88.6 us
    pallas_call x1, Pallas kernels, gather_and_pick(): pl.pallas_call(functools.partial(gather_kernel, n, heads, nope), grid=(st...  49.1 us
    pallas_call x1, Pallas kernels, latents(): pl.pallas_call(functools.partial(latent_kernel, kv_rank), in_specs=[anysp...  14.7 us
    all_to_all x2, starting transfers between devices, local_step(): o_parts.append(lax.all_to_all(o_g, 'sp', 0, 0, tiled=True))  9.91 us
  transfers between devices with their start and end apart: 2, of which 1 were waited for; matrix products, arithmetic and copies ran while one was open for 0% of the time, Pallas kernels for 35%

profile of v6, /device:TPU:81, one launch (start us, length us, event | category | flops | bytes accessed | tf_op | source)
XLA Modules:
  0.0 271.5 jit_solution(13912616929407339012)
XLA Ops:
  0.6 0.7 convert_element_type.3
  1.3 0.9 multiply_cosine_fusion
  2.2 0.6 pad_maximum_fusion.cs_ref
  2.8 14.7 %latents.1 = (bf16[256,1536]{1,0:T(8,128)(2,1)}, bf16[256,512]{1,0:T(8,128)(2,1)}, bf16[256,64]{1,0:T(8,128)(2,1)}, bf16[256,640]{1,0:T(8,128)(2,1)}) custom-call(bf16[256,7168]{1,0:T(8,128)(2,1)} %x_ref.1, bf16[7168,1536]{1,0:T(8,128)(2,1)} %wq_ref.1, bf16[576,7168]{1,0:T(8,128)(2,1)} %bitcast.7, f32[1536]{0:T(1024)} %gq_ref.1, f32[512]{0:T(512)} %gkv_ref.1, ...), custom_call_target="tpu_custom_call" | custom-call | flops 7751073792 | bytes 33947648 | tf_op jit(solution)/shard_map/latents/pallas_call | solution.py:113
  17.5 49.1 %gather_pick.1 = (bf16[2048,640]{1,0:T(8,128)(2,1)}, f32[512,256]{1,0:T(8,128)}, bf16[2048,1536]{1,0:T(8,128)(2,1)}, bf16[1536,2048]{1,0:T(8,128)(2,1)}, bf16[15...) custom-call(bf16[256,640]{1,0:T(8,128)(2,1)} %get-tuple-element.14.kv_ref, ...), custom_call_target="tpu_custom_call" | custom-call | flops 30000001024 | bytes 90000000 | tf_op jit(solution)/shard_map/gather_pick/pallas_call | solution.py:284
  66.6 50.7 %mla_attn.2 = bf16[2048,1024]{1,0:T(8,128)(2,1)} custom-call(bf16[2048,640]{1,0:T(8,128)(2,1)} %get-tuple-element.16.kv_ref, bf16[2048,1536]{1,0:T(8,128)(2,1)} %get-tuple-element.17.cq_ref, f32[512,256]{1,0:T(8,128)} %get-tuple-element.18.cs_ref, bf16[1536,2048]{1,0:T(8,128)(2,1)} %get-tuple-element.19.wn_hbm, bf16[1536,1024]{1,0:T(8,128)(2,1)} %get-tuple-element.20.wr_hbm, ...), custom_call_target="tpu_custom_call" | custom-call | flops 40802189312 | bytes 12000000 | tf_op jit(solution)/shard_map/mla_attn/pallas_call | solution.py:486
  117.4 4.9 %all-to-all-start = ((bf16[8,256,1024]{2,1,0:T(8,128)(2,1)}), bf16[8,256,1024]{2,1,0:T(8,128)(2,1)}, u32[]{:S(2)}, u32[]{:S(2)}) async-start(bf16[8,256,1024]{2,1,0:T(8,128)(2,1)} %bitcast.9), calls=%async_computation | async-start | bytes 8388608 | tf_op jit(solution)/shard_map/all_to_all | solution.py:626
  122.3 50.5 %mla_attn.3 = bf16[2048,1024]{1,0:T(8,128)(2,1)} custom-call(bf16[2048,640]{1,0:T(8,128)(2,1)} %get-tuple-element.16.kv_ref, bf16[2048,1536]{1,0:T(8,128)(2,1)} %get-tuple-element.17.cq_ref, f32[512,256]{1,0:T(8,128)} %get-tuple-element.18.cs_ref, bf16[1536,2048]{1,0:T(8,128)(2,1)} %get-tuple-element.19.wn_hbm, bf16[1536,1024]{1,0:T(8,128)(2,1)} %get-tuple-element.20.wr_hbm, ...), custom_call_target="tpu_custom_call" | custom-call | flops 40802189312 | bytes 12000000 | tf_op jit(solution)/shard_map/mla_attn/pallas_call | solution.py:486
  172.8 0.0 all-to-all-done
  172.8 0.0 copy-start
  172.8 5.0 %all-to-all-start.1 = ((bf16[8,256,1024]{2,1,0:T(8,128)(2,1)}), bf16[8,256,1024]{2,1,0:T(8,128)(2,1)}, u32[]{:S(2)}, u32[]{:S(2)}) async-start(bf16[8,256,1024]{2,1,0:T(8,128)(2,1)} %bitcast.8), calls=%async_computation.1 | async-start | bytes 8388608 | tf_op jit(solution)/shard_map/all_to_all | solution.py:626
  177.9 0.0 copy-done
  177.9 0.7 copy.14
  178.6 43.6 %out_product.2.refs_0_ = f32[4,256,1792]{2,1,0:T(8,128)} custom-call(bf16[2048,1024]{1,0:T(8,128)(2,1)} %bitcast.3.refs_0_, bf16[8,2,1024,7168]{3,2,1,0:T(8,128)(2,1)} %bitcast.4.refs_1_.refs_2_), custom_call_target="tpu_custom_call" | custom-call | flops 30064771072 | bytes 117440512 | tf_op jit(solution)/shard_map/out_product/pallas_call | solution.py:581
  222.2 4.2 %all-to-all-done.1 = bf16[8,256,1024]{2,1,0:T(8,128)(2,1)} async-done(((bf16[8,256,1024]{2,1,0:T(8,128)(2,1)}), bf16[8,256,1024]{2,1,0:T(8,128)(2,1)}, u32[]{:S(2)}, u32[]{:S(2)}) %all-to-all-start.1) | async-done | bytes 4194336 | tf_op jit(solution)/shard_map/all_to_all | solution.py:626
  226.3 45.0 %out_product.3 = bf16[256,7168]{1,0:T(8,128)(2,1)} custom-call(f32[4,256,1792]{2,1,0:T(8,128)} %out_product.2.refs_0_, bf16[2048,1024]{1,0:T(8,128)(2,1)} %bitcast.6.refs_1_, bf16[8,2,1024,7168]{3,2,1,0:T(8,128)(2,1)} %bitcast.4.refs_1_.refs_2_), custom_call_target="tpu_custom_call" | custom-call | flops 30064771072 | bytes 117440512 | tf_op jit(solution)/shard_map/out_product/pallas_call | solution.py:581
Async XLA Ops:
  117.4 55.4 %all-to-all-start = ((bf16[8,256,1024]{2,1,0:T(8,128)(2,1)}), bf16[8,256,1024]{2,1,0:T(8,128)(2,1)}, u32[]{:S(2)}, u32[]{:S(2)}) async-start(bf16[8,256,1024]{2,1,0:T(8,128)(2,1)} %bitcast.9), calls=%async_computation | async-start | bytes 8388608 | tf_op jit(solution)/shard_map/all_to_all | solution.py:626
  172.8 5.1 %copy-start = (bf16[256,64]{1,0:T(8,128)(2,1)S(1)}, bf16[256,64]{1,0:T(8,128)(2,1)}, u32[]{:S(2)}) copy-start(bf16[256,64]{1,0:T(8,128)(2,1)} %get-tuple-element.27) | copy-start | bytes 98308
  172.8 53.5 %all-to-all-start.1 = ((bf16[8,256,1024]{2,1,0:T(8,128)(2,1)}), bf16[8,256,1024]{2,1,0:T(8,128)(2,1)}, u32[]{:S(2)}, u32[]{:S(2)}) async-start(bf16[8,256,1024]{2,1,0:T(8,128)(2,1)} %bitcast.8), calls=%async_computation.1 | async-start | bytes 8388608 | tf_op jit(solution)/shard_map/all_to_all | solution.py:626
